TPU v7x, 8 devices: a whole 2x2x1 slice. The times are simulated.
8 devices in a mesh: dp: 1 (over z), tp: 8 (over y, x, core).
Axes of the slice: x: 2, y: 2, z: 1, core: 2. Of those that a mesh axis runs over, the one named last changes fastest.
Arguments:
- tokens: bfloat16 [1, 4096, 3584], P('dp', 'tp')
- start_pos: int32 [1], P('dp')
- cos_tab: float32 [1, 4096, 256], P('dp')
- sin_tab: float32 [1, 4096, 256], P('dp')
- key_cache: bfloat16 [2, 1, 4096, 8, 256], P(None, 'dp', None, 'tp')
- value_cache: bfloat16 [2, 1, 4096, 8, 256], P(None, 'dp', None, 'tp')
- slot_pos: int32 [1, 4096], P('dp')
- norm_params: bfloat16 [2, 4, 3584], replicated
- w_q: bfloat16 [2, 3584, 4096], P(None, None, 'tp')
- b_q: bfloat16 [2, 4096], P(None, 'tp')
- w_k: bfloat16 [2, 3584, 2048], P(None, None, 'tp')
- b_k: bfloat16 [2, 2048], P(None, 'tp')
- w_v: bfloat16 [2, 3584, 2048], P(None, None, 'tp')
- b_v: bfloat16 [2, 2048], P(None, 'tp')
- w_o: bfloat16 [2, 4096, 3584], P(None, 'tp')
- b_o: bfloat16 [2, 3584], replicated
- w_up: bfloat16 [2, 3584, 14336], P(None, None, 'tp')
- b_up: bfloat16 [2, 14336], P(None, 'tp')
- w_down: bfloat16 [2, 14336, 3584], P(None, 'tp')
- b_down: bfloat16 [2, 3584], replicated
Outputs:
- output 1: bfloat16 [1, 4096, 3584], P('dp', 'tp')
- output 2: bfloat16 [2, 1, 4096, 8, 256], P(None, 'dp', None, 'tp')
- output 3: bfloat16 [2, 1, 4096, 8, 256], P(None, 'dp', None, 'tp')
- output 4: int32 [1, 4096], P('dp')
All inputs are finite; a program needn't handle non-finite values.
Results may differ from a plain program's by a relative error of at most 0.0194662.
Values are sent between devices in bfloat16 or wider.
A program may use at most 1 GiB of HBM per device.

v0:
```python
import functools

import jax
import jax.numpy as jnp
from jax import lax
from jax.experimental import pallas as pl
from jax.experimental.pallas import tpu as pltpu
from jax.sharding import PartitionSpec as P

NORM_EPS = 1e-5
LOG2E = 1.4426950408889634
CHUNKS = 4
KEY_TILE = 512
LANES = 128
WIDE = 512
ROW_BLOCK = 16
WEIGHT_SLOTS = 3
ROLL_ROWS = 256
VMEM_LIMIT = 62 * 1024 * 1024
BF16 = jnp.bfloat16
F32 = jnp.float32
MESH = pl.DeviceIdType.MESH

ANY = pl.BlockSpec(memory_space=pl.ANY)
SMEM = pl.BlockSpec(memory_space=pltpu.SMEM)
VMEM = pl.BlockSpec(memory_space=pltpu.VMEM)
DMA = pltpu.SemaphoreType.DMA


def gelu_tanh(x):
    inner = 0.7978845608028654 * (x + 0.044715 * (x * x * x))
    return 0.5 * x * (1.0 + jnp.tanh(inner))


def normalized(values, gain, shift):
    centered = values - jnp.mean(values, axis=-1, keepdims=True)
    variance = jnp.mean(centered * centered, axis=-1, keepdims=True)
    return (centered * lax.rsqrt(variance + NORM_EPS) * gain + shift).astype(BF16)


def rotate(src, dst, shift, first, last):
    window = src.shape[1]

    def tile(n, carry):
        at = pl.multiple_of(n * ROLL_ROWS, ROLL_ROWS)
        want = lax.broadcasted_iota(jnp.int32, (ROLL_ROWS, 1), 0) + (n * ROLL_ROWS + shift)
        want = jnp.where(want >= window, want - window, want)
        pick = jnp.where(lax.broadcasted_iota(jnp.int32, (1, window), 1) == want, 1.0, 0.0).astype(BF16)
        for k in range(2):
            dst[k, pl.ds(at, ROLL_ROWS), :] = jnp.dot(pick, src[k], preferred_element_type=F32).astype(BF16)
        return carry

    lax.fori_loop(first, last, tile, 0)


class Place:
    def __init__(self):
        me = lax.axis_index('tp')
        self.core = lax.rem(me, 2)
        self.xb = lax.rem(lax.div(me, 2), 2)
        self.yb = lax.div(me, 4)
        self.peer = me + 1 - 2 * self.core
        self.x = me + 2 - 4 * self.xb
        self.y = me + 4 - 8 * self.yb

    def member(self, i):
        xb = self.xb + lax.rem(i, 2) * (1 - 2 * self.xb)
        yb = self.yb + lax.div(i, 2) * (1 - 2 * self.yb)
        return yb * 2 + xb

    def barrier(self, others):
        sem = pltpu.get_barrier_semaphore()
        for other in others:
            pl.semaphore_signal(sem, inc=1, device_id={'tp': other}, device_id_type=MESH)
        pl.semaphore_wait(sem, len(others))


def remote(src, dst, send_sem, recv_sem, other):
    return pltpu.make_async_remote_copy(src_ref=src, dst_ref=dst, send_sem=send_sem, recv_sem=recv_sem, device_id={'tp': other}, device_id_type=MESH)


class Gather:
    def __init__(self, place, x_s, send, recv, rows):
        self.place, self.x_s, self.send, self.recv, self.rows = place, x_s, send, recv, rows

    def copy(self, c, kind):
        r, h = self.rows, self.rows // 2
        src, dst, size, other = ((0, r, r, self.place.x), (0, 2 * r, r, self.place.y), (r, 3 * r, h, self.place.y), (2 * r + h, 3 * r + h, h, self.place.x))[kind]
        return remote(self.x_s.at[c, pl.ds(src, size)], self.x_s.at[c, pl.ds(dst, size)], self.send.at[c, kind], self.recv.at[c, kind], other)

    def start(self, c):
        self.copy(c, 0).start()
        self.copy(c, 1).start()

    def forward(self, c):
        self.copy(c, 0).wait_recv()
        self.copy(c, 2).start()
        self.copy(c, 1).wait_recv()
        self.copy(c, 3).start()

    def finish(self, c):
        self.copy(c, 2).wait_recv()
        self.copy(c, 3).wait_recv()

    def drain(self, c):
        for kind in range(4):
            self.copy(c, kind).wait_send()


class Scatter:
    def __init__(self, place, out_s, land_s, send, recv, rows):
        self.place, self.out_s, self.land_s, self.send, self.recv, self.rows = place, out_s, land_s, send, recv, rows

    def copy(self, c, kind):
        r, h = self.rows, self.rows // 2
        x, y = self.place.x, self.place.y
        src, dst, other = ((3 * r, 2 * r, x), (3 * r + h, 2 * r + h, y), (r, 0, x), (2 * r + h, r + h, y), (r + h, h, x), (2 * r, r, y))[kind]
        return remote(self.out_s.at[c, pl.ds(src, h)], self.land_s.at[c, pl.ds(dst, h)], self.send.at[c, kind], self.recv.at[c, kind], other)

    def start(self, c):
        for kind in range(4):
            self.copy(c, kind).start()

    def add(self, c, kind, src, dst):
        self.copy(c, kind).wait_recv()

        def block(n, carry):
            at = pl.multiple_of(n * ROW_BLOCK, ROW_BLOCK)
            mine = self.out_s[c, pl.ds(dst + at, ROW_BLOCK), :].astype(F32)
            came = self.land_s[c, pl.ds(src + at, ROW_BLOCK), :].astype(F32)
            self.out_s[c, pl.ds(dst + at, ROW_BLOCK), :] = (mine + came).astype(BF16)
            return carry

        lax.fori_loop(0, self.rows // 2 // ROW_BLOCK, block, 0)

    def relay(self, c):
        r, h = self.rows, self.rows // 2
        self.add(c, 0, 2 * r, 2 * r)
        self.copy(c, 5).start()
        self.add(c, 1, 2 * r + h, r + h)
        self.copy(c, 4).start()

    def finish(self, c):
        for kind in range(2, 6):
            self.copy(c, kind).wait_recv()

    def close(self, mid_s, bias, out, o_sem, chunks, first_open):
        rows = self.rows

        def o_copy(c):
            return pltpu.make_async_copy(mid_s.at[c], out.at[pl.ds(pl.multiple_of(c * rows, rows), rows)], o_sem.at[c])

        def one(c, carry):
            @pl.when(c + first_open < chunks)
            def _():
                self.relay(c + first_open)

            self.finish(c)

            def block(n, inner):
                at = pl.multiple_of(n * ROW_BLOCK, ROW_BLOCK)
                total = self.out_s[c, pl.ds(at, ROW_BLOCK), :].astype(F32) + self.land_s[c, pl.ds(at, ROW_BLOCK), :].astype(F32) + self.land_s[c, pl.ds(rows + at, ROW_BLOCK), :].astype(F32)
                mid_s[c, pl.ds(at, ROW_BLOCK), :] = (mid_s[c, pl.ds(at, ROW_BLOCK), :].astype(F32) + total + bias).astype(BF16)
                return inner

            lax.fori_loop(0, rows // ROW_BLOCK, block, 0)
            o_copy(c).start()
            return carry

        lax.fori_loop(0, chunks, one, 0)

        def settle(c, carry):
            o_copy(c).wait()
            for kind in range(6):
                self.copy(c, kind).wait_send()
            return carry

        lax.fori_loop(0, chunks, settle, 0)


def qkv_kernel(layer, dims, scal, *refs):
    chunks, rows, model, hd, window = dims
    hidden, norms, cos, sin, wq, wk, wv, biases, b_all = refs[:9]
    pushed = refs[9:14]
    q_out, kv_mine, kv_other, cache_mine, cache_peer, wo_peer, up_peer, down_peer = refs[14:22]
    x_s, h_s, t_s, w_s, b_s, bp_s, oq_s, okv_s, raw_s, old_s, ag_send, ag_recv, h_sem, t_sem, w_sem, wr_send, wr_recv, p_send, p_recv, q_sem, kv_sem, kr_send, kr_recv, raw_sem, old_sem = refs[22:]
    place = Place()
    block = rows * chunks
    place.barrier((place.x, place.y, place.peer))
    gather = Gather(place, x_s, ag_send, ag_recv, rows)
    loads = [pltpu.make_async_copy(hidden.at[pl.ds(c * rows, rows)], h_s.at[c], h_sem.at[c]) for c in range(chunks)]
    for copy in loads:
        copy.start()
    for k in range(2):
        pltpu.make_async_copy(pushed[k].at[layer], raw_s.at[k], raw_sem).start()
    places = ((wq.at[layer], 0, 0, 2 * hd), (wk.at[layer], 1, 0, hd), (wv.at[layer], 1, hd, hd))
    w_local = [pltpu.make_async_copy(src, w_s.at[t, :, pl.ds(at, n)], w_sem.at[k]) for k, (src, t, at, n) in enumerate(places)]
    w_remote = [remote(src, w_s.at[2 + t, :, pl.ds(at, n)], wr_send.at[k], wr_recv.at[k], place.peer) for k, (src, t, at, n) in enumerate(places)]
    w_remote.append(remote(b_all, bp_s, wr_send.at[3], wr_recv.at[3], place.peer))
    landing = (wo_peer, up_peer, down_peer)
    pushes = [remote(src.at[layer], dst, p_send.at[k], p_recv.at[k], place.peer) for k, (src, dst) in enumerate(zip(pushed[2:], landing))]
    old_push = remote(old_s, cache_peer, p_send.at[3], p_recv.at[3], place.peer)
    old_store = pltpu.make_async_copy(old_s, cache_mine, old_sem)
    gain = norms[layer, 0:1, :].astype(F32)
    shift = norms[layer, 1:2, :].astype(F32)

    def send_own(c):
        loads[c].wait()

        def norm_block(n, carry):
            at = pl.multiple_of(n * ROW_BLOCK, ROW_BLOCK)
            x_s[c, pl.ds(at, ROW_BLOCK), :] = normalized(h_s[c, pl.ds(at, ROW_BLOCK), :].astype(F32), gain, shift)
            return carry

        lax.fori_loop(0, rows // ROW_BLOCK, norm_block, 0)
        gather.start(c)

    def chunk_pos(c, i):
        return pl.multiple_of((place.member(i) * 2 + place.core) * block + c * rows, rows)

    def table_copies(c):
        return [pltpu.make_async_copy(tab.at[pl.ds(chunk_pos(c, i), rows)], t_s.at[c, k, pl.ds(i * rows, rows)], t_sem.at[c]) for i in range(4) for k, tab in enumerate((cos, sin))]

    send_own(0)
    send_own(1)
    for copy in w_remote + w_local + pushes:
        copy.start()
    for c in range(chunks):
        for copy in table_copies(c):
            copy.start()
    b_s[0] = biases[layer:layer + 1, 0:2 * hd].astype(F32)
    b_s[1] = biases[layer:layer + 1, 2 * hd:4 * hd].astype(F32)
    pltpu.make_async_copy(raw_s, raw_s, raw_sem).wait()
    first_slot = lax.rem(scal[0], window)
    roll_tiles = window // ROLL_ROWS
    rotate(raw_s, old_s, first_slot, 0, roll_tiles // 3)
    gather.forward(0)
    send_own(2)
    rotate(raw_s, old_s, first_slot, roll_tiles // 3, roll_tiles)
    old_push.start()
    old_store.start()
    gather.forward(1)
    send_own(3)
    w_remote[3].wait_recv()
    b_s[2] = bp_s[layer:layer + 1, 0:2 * hd].astype(F32)
    b_s[3] = bp_s[layer:layer + 1, 2 * hd:4 * hd].astype(F32)

    def rope(u, c):
        turned = jnp.concatenate([-u[:, hd // 2:], u[:, :hd // 2]], axis=1)
        return (u * t_s[c, 0] + turned * t_s[c, 1]).astype(BF16).reshape(4, rows, hd)

    def q_copy(c):
        return pltpu.make_async_copy(oq_s.at[c], q_out.at[c], q_sem.at[c])

    def kv_copies(c):
        planes = (kv_mine, kv_other)
        near = [pltpu.make_async_copy(okv_s.at[c, :, g, i], planes[g].at[:, pl.ds(chunk_pos(c, i), rows)], kv_sem.at[c]) for g in range(2) for i in range(4)]
        far = [remote(okv_s.at[c, :, g, i], planes[1 - g].at[:, pl.ds(chunk_pos(c, i), rows)], kr_send.at[c], kr_recv.at[c], place.peer) for g in range(2) for i in range(4)]
        return near, far

    def chunk(c, carry):
        pltpu.make_async_copy(t_s.at[c], t_s.at[c], t_sem.at[c]).wait()
        gather.finish(c)
        for g in range(2):
            @pl.when(c == 0)
            def _():
                for copy in ((w_local[0],) if g == 0 else ()):
                    copy.wait()
                if g == 1:
                    w_remote[0].wait_recv()

            u = jnp.dot(x_s[c], w_s[2 * g], preferred_element_type=F32) + b_s[2 * g]
            for h in range(2):
                oq_s[c, g, :, h] = rope(u[:, h * hd:(h + 1) * hd], c)

            @pl.when(c == 0)
            def _():
                for copy in (w_local[1:] if g == 0 else ()):
                    copy.wait()
                if g == 1:
                    for copy in w_remote[1:3]:
                        copy.wait_recv()

            u = jnp.dot(x_s[c], w_s[2 * g + 1], preferred_element_type=F32) + b_s[2 * g + 1]
            okv_s[c, 0, g] = rope(u[:, :hd], c)
            okv_s[c, 1, g] = u[:, hd:].astype(BF16).reshape(4, rows, hd)
        q_copy(c).start()
        near, far = kv_copies(c)
        for copy in near + far:
            copy.start()

        @pl.when(c + 2 < chunks)
        def _():
            gather.forward(c + 2)

        return carry

    lax.fori_loop(0, chunks, chunk, 0)
    for copy in w_remote:
        copy.wait_send()

    def settle(c, carry):
        q_copy(c).wait()
        whole = okv_s.at[c]
        pltpu.make_async_copy(whole, whole, kv_sem.at[c]).wait()
        remote(whole, whole, kr_send.at[c], kr_recv.at[c], place.peer).wait_send()
        remote(whole, whole, kr_send.at[c], kr_recv.at[c], place.peer).wait_recv()
        gather.drain(c)
        return carry

    lax.fori_loop(0, chunks, settle, 0)
    for copy in pushes + [old_push]:
        copy.wait_send()
        copy.wait_recv()
    old_store.wait()


def run_qkv(layer, chunks, scal, hidden, norms, cos, sin, weights, b_all, pushed):
    model = hidden.shape[1]
    rows = hidden.shape[0] // chunks
    hd = cos.shape[1]
    window = cos.shape[0]
    dims = (chunks, rows, model, hd, window)
    flops = 2 * 4 * rows * chunks * model * 8 * hd
    shapes = [(chunks, 2, 4, 2, rows, hd)] + [(2, window, hd)] * 4 + [p.shape[1:] for p in pushed[2:]]
    return pl.pallas_call(
        functools.partial(qkv_kernel, layer, dims),
        out_shape=tuple(jax.ShapeDtypeStruct(s, BF16) for s in shapes),
        in_specs=[SMEM, ANY, VMEM] + [ANY] * 5 + [VMEM] + [ANY] * 6,
        out_specs=(ANY,) * len(shapes),
        scratch_shapes=[
            pltpu.VMEM((chunks, 4 * rows, model), BF16),
            pltpu.VMEM((chunks, rows, model), BF16),
            pltpu.VMEM((chunks, 2, 4 * rows, hd), F32),
            pltpu.VMEM((4, model, 2 * hd), BF16),
            pltpu.VMEM((4, 1, 2 * hd), F32),
            pltpu.VMEM(b_all.shape, BF16),
            pltpu.VMEM((chunks, 2, 4, 2, rows, hd), BF16),
            pltpu.VMEM((chunks, 2, 2, 4, rows, hd), BF16),
            pltpu.VMEM((2, window, hd), BF16),
            pltpu.VMEM((2, window, hd), BF16),
            DMA((chunks, 4)),
            DMA((chunks, 4)),
            DMA((chunks,)),
            DMA((chunks,)),
            DMA((3,)),
            DMA((4,)),
            DMA((4,)),
            DMA((4,)),
            DMA((4,)),
            DMA((chunks,)),
            DMA((chunks,)),
            DMA((chunks,)),
            DMA((chunks,)),
            DMA,
            DMA,
        ],
        compiler_params=pltpu.CompilerParams(vmem_limit_bytes=VMEM_LIMIT, collective_id=3 * layer, has_side_effects=True),
        cost_estimate=pl.CostEstimate(flops=4 * flops, bytes_accessed=20_000_000, transcendentals=0),
        name=f"qkv_l{layer}",
    )(scal, hidden, norms, cos, sin, *weights, b_all, b_all, *pushed)


def attn_kernel(layer, dims, scal, *refs):
    chunks, rows, model, hd, window = dims
    q, kv_mine, kv_other, cache_mine, cache_peer, wo, wo_peer, hidden, b_o = refs[:9]
    mid_out, kv_rolled = refs[9:11]
    kv_s, q_s, s_s, mix_s, wo_s, out_s, land_s, mid_s, m_s, l_s, acc_s, rs_send, rs_recv, kv_sem, q_sem, w_sem, h_sem, o_sem, f_sem = refs[11:]
    place = Place()
    start_pos = scal[0]
    block = rows * chunks
    tall = 2 * rows
    tile = KEY_TILE
    tiles = window // tile
    scale = LOG2E * hd ** -0.5
    place.barrier((place.x, place.y))
    scatter = Scatter(place, out_s, land_s, rs_send, rs_recv, rows)
    q_load = pltpu.make_async_copy(q, q_s, q_sem)
    q_load.start()
    pltpu.make_async_copy(kv_mine, kv_s.at[0, pl.ds(2, 2)], kv_sem).start()
    pltpu.make_async_copy(kv_other, kv_s.at[1, pl.ds(2, 2)], kv_sem).start()
    pltpu.make_async_copy(cache_mine, kv_s.at[0, pl.ds(0, 2)], kv_sem).start()
    pltpu.make_async_copy(cache_peer, kv_s.at[1, pl.ds(0, 2)], kv_sem).start()
    pltpu.make_async_copy(wo.at[layer], wo_s.at[pl.ds(0, 2 * hd)], w_sem).start()
    pltpu.make_async_copy(wo_peer, wo_s.at[pl.ds(2 * hd, 2 * hd)], w_sem).start()
    for c in range(chunks):
        pltpu.make_async_copy(hidden.at[pl.ds(c * rows, rows)], mid_s.at[c], h_sem).start()
    q_load.wait()
    pltpu.make_async_copy(kv_s, kv_s, kv_sem).wait()
    first_slot = lax.rem(start_pos, window)
    floor = window - 1 - start_pos

    def first_row(c, i):
        return (place.member(i) * 2 + place.core) * block + c * rows

    def tile_at(diag, n):
        is_new = jnp.logical_or(n == 0, jnp.logical_and(n >= 2, n - 2 < diag))
        t = jnp.where(n < 2, diag, jnp.where(is_new, n - 2, n - 1))
        return jnp.where(is_new, 2, 0), pl.multiple_of(t * tile, tile), is_new

    def scores(c, i, g, which, at):
        return lax.dot_general(q_s[c, g, i].reshape(tall, hd), kv_s[g, which, pl.ds(at, tile), :], (((1,), (1,)), ((), ())), preferred_element_type=F32)

    for g in range(2):
        s_s[g] = scores(0, 0, g, 2, pl.multiple_of(lax.div(first_row(0, 0), tile) * tile, tile))

    def attend(c, i):
        j0 = first_row(c, i)
        diag = lax.div(j0, tile)
        count = tiles + 1
        end = i == 3
        c_next = jnp.minimum(jnp.where(end, c + 1, c), chunks - 1)
        i_next = jnp.where(end, 0, i + 1)
        next_at = lax.div(first_row(c_next, i_next), tile) * tile
        m_s[...] = jnp.full_like(m_s, -jnp.inf)
        l_s[...] = jnp.zeros_like(l_s)
        acc_s[...] = jnp.zeros_like(acc_s)

        def step(n):
            if isinstance(n, int):
                which, at = (2, 0)[n], pl.multiple_of(diag * tile, tile)
                nw, nat, _ = (0, at, None) if n == 0 else tile_at(diag, 2)
                nc, ni = c, i
                col = lax.broadcasted_iota(jnp.int32, (1, tile), 1) + at
                row = lax.rem(lax.broadcasted_iota(jnp.int32, (tall, 1), 0), rows) + j0
                mask = col <= row if n == 0 else col > jnp.maximum(row, floor)
            else:
                which, at, is_new = tile_at(diag, n)
                last = n + 1 == count
                nw, nat, _ = tile_at(diag, n + 1)
                nw = jnp.where(last, 2, nw)
                nat = pl.multiple_of(jnp.where(last, next_at, nat), tile)
                nc = jnp.where(last, c_next, c)
                ni = jnp.where(last, i_next, i)
                col = lax.broadcasted_iota(jnp.int32, (1, tile), 1) + at
                mask = col > jnp.where(is_new, -1, floor)
            for g in range(2):
                s = jnp.where(mask, s_s[g] * scale, -jnp.inf)
                s_next = scores(nc, ni, g, nw, nat)
                m_prev = m_s[g]
                m_next = jnp.maximum(m_prev, jnp.max(s, axis=1, keepdims=True))
                e = jnp.exp2(s - jnp.concatenate([m_next] * (tile // LANES), axis=1))
                alpha = jnp.exp2(m_prev - m_next)
                total = l_s[g] * alpha
                for k in range(tile // LANES):
                    total = total + e[:, k * LANES:(k + 1) * LANES]
                l_s[g] = total
                m_s[g] = m_next
                mixed = jnp.dot(e.astype(BF16), kv_s[g, which + 1, pl.ds(at, tile), :], preferred_element_type=F32)
                acc_s[g] = acc_s[g] * jnp.concatenate([alpha] * (hd // LANES), axis=1) + mixed
                s_s[g] = s_next

        step(0)
        step(1)
        lax.fori_loop(2, count, lambda n, x: (step(n), x)[1], 0)
        at = pl.multiple_of(i * rows, rows)
        for g in range(2):
            total = jnp.sum(l_s[g], axis=1, keepdims=True)
            out = (acc_s[g] / total).astype(BF16)
            for h in range(2):
                mix_s[pl.ds(at, rows), (2 * g + h) * hd:(2 * g + h + 1) * hd] = out[h * rows:(h + 1) * rows]

    def chunk(c, carry):
        def one(i, inner):
            attend(c, i)

            @pl.when(jnp.logical_and(i == 2, c >= 1))
            def _():
                scatter.relay(c - 1)

            return inner

        lax.fori_loop(0, 4, one, 0)

        @pl.when(c == 0)
        def _():
            pltpu.make_async_copy(wo_s, wo_s, w_sem).wait()

        def project(n, inner):
            at = pl.multiple_of(n * WIDE, WIDE)
            out_s[c, :, pl.ds(at, WIDE)] = jnp.dot(mix_s[...], wo_s[:, pl.ds(at, WIDE)], preferred_element_type=F32).astype(BF16)
            return inner

        lax.fori_loop(0, model // WIDE, project, 0)
        scatter.start(c)
        return carry

    lax.fori_loop(0, chunks, chunk, 0)
    pltpu.make_async_copy(mid_s, mid_s, h_sem).wait()
    rolled = kv_s.at[1, pl.ds(0, 2)]
    rotate(kv_s.at[0, pl.ds(2, 2)], rolled, window - first_slot, 0, window // ROLL_ROWS)
    roll_store = pltpu.make_async_copy(rolled, kv_rolled, f_sem)
    roll_store.start()
    scatter.close(mid_s, b_o[layer:layer + 1, :].astype(F32), mid_out, o_sem, chunks, chunks - 1)
    roll_store.wait()


def run_attn(layer, scal, q, kv_mine, kv_other, cache_mine, cache_peer, wo, wo_peer, hidden, b_o):
    chunks, rows, hd = q.shape[0], q.shape[-2], q.shape[-1]
    model = hidden.shape[1]
    window = kv_mine.shape[1]
    dims = (chunks, rows, model, hd, window)
    flops = 4 * 4 * rows * chunks * 4 * window * hd + 2 * 4 * rows * chunks * 4 * hd * model
    return pl.pallas_call(
        functools.partial(attn_kernel, layer, dims),
        out_shape=(jax.ShapeDtypeStruct(hidden.shape, BF16), jax.ShapeDtypeStruct((2, window, hd), BF16)),
        in_specs=[SMEM] + [ANY] * 8 + [VMEM],
        out_specs=(ANY, ANY),
        scratch_shapes=[
            pltpu.VMEM((2, 4, window, hd), BF16),
            pltpu.VMEM((chunks, 2, 4, 2, rows, hd), BF16),
            pltpu.VMEM((2, 2 * rows, KEY_TILE), F32),
            pltpu.VMEM((4 * rows, 4 * hd), BF16),
            pltpu.VMEM((4 * hd, model), BF16),
            pltpu.VMEM((chunks, 4 * rows, model), BF16),
            pltpu.VMEM((chunks, 3 * rows, model), BF16),
            pltpu.VMEM((chunks, rows, model), BF16),
            pltpu.VMEM((2, 2 * rows, LANES), F32),
            pltpu.VMEM((2, 2 * rows, LANES), F32),
            pltpu.VMEM((2, 2 * rows, hd), F32),
            DMA((chunks, 6)),
            DMA((chunks, 6)),
            DMA,
            DMA,
            DMA,
            DMA,
            DMA((chunks,)),
            DMA,
        ],
        compiler_params=pltpu.CompilerParams(vmem_limit_bytes=VMEM_LIMIT, collective_id=3 * layer + 1, has_side_effects=True),
        cost_estimate=pl.CostEstimate(flops=flops, bytes_accessed=30_000_000, transcendentals=16 * rows * chunks * window),
        name=f"attn_l{layer}",
    )(scal, q, kv_mine, kv_other, cache_mine, cache_peer, wo, wo_peer, hidden, b_o)


def mlp_kernel(layer, dims, bias_at, *refs):
    chunks, rows, model, ffn = dims
    middle, norms, b_down, biases, b_all, up, down, up_peer, down_peer = refs[:9]
    h_out = refs[9]
    x_s, out_s, land_s, act_s, w_s, mid_s, b_s, bp_s, ag_send, ag_recv, rs_send, rs_recv, m_sem, w_sem, b_send, b_recv, h_sem = refs[10:]
    place = Place()
    n_up = 2 * ffn // WIDE
    n_tiles = n_up + model // WIDE
    sub = WIDE // 2
    n_sub = ffn // sub
    ups = (up.at[layer], up_peer)
    downs = (down.at[layer], down_peer)
    loads = [pltpu.make_async_copy(middle.at[pl.ds(c * rows, rows)], mid_s.at[c], m_sem.at[c]) for c in range(chunks)]
    for copy in loads:
        copy.start()
    place.barrier((place.x, place.y, place.peer))
    gather = Gather(place, x_s, ag_send, ag_recv, rows)
    scatter = Scatter(place, out_s, land_s, rs_send, rs_recv, rows)
    gain = norms[layer, 2:3, :].astype(F32)
    shift = norms[layer, 3:4, :].astype(F32)

    def fetch(c, k):
        over = k >= n_tiles
        k = jnp.where(over, k - n_tiles, k)
        c = jnp.where(over, c + 1, c)
        slot = lax.rem(c * n_tiles + k, WEIGHT_SLOTS)

        @pl.when(c < chunks)
        def _():
            for part in range(2):
                n = 2 * k + part
                for side in range(2):
                    @pl.when(jnp.logical_and(n >= side * n_sub, n < (side + 1) * n_sub))
                    def _():
                        at = pl.multiple_of((n - side * n_sub) * sub, sub)
                        pltpu.make_async_copy(ups[side].at[:, pl.ds(at, sub)], w_s.at[slot, :, pl.ds(part * sub, sub)], w_sem.at[slot]).start()

            @pl.when(k >= n_up)
            def _():
                at = pl.multiple_of((k - n_up) * WIDE, WIDE)
                for side in range(2):
                    pltpu.make_async_copy(downs[side].at[:, pl.ds(at, WIDE)], w_s.at[slot, pl.ds(side * ffn, ffn)], w_sem.at[slot]).start()

    def landed(c, k):
        slot = lax.rem(c * n_tiles + k, WEIGHT_SLOTS)
        pltpu.make_async_copy(w_s.at[slot], w_s.at[slot], w_sem.at[slot]).wait()
        fetch(c, k + WEIGHT_SLOTS - 1)
        return slot

    def send_own(c):
        loads[c].wait()

        def norm_block(n, carry):
            at = pl.multiple_of(n * ROW_BLOCK, ROW_BLOCK)
            x_s[c, pl.ds(at, ROW_BLOCK), :] = normalized(mid_s[c, pl.ds(at, ROW_BLOCK), :].astype(F32), gain, shift)
            return carry

        lax.fori_loop(0, rows // ROW_BLOCK, norm_block, 0)
        gather.start(c)

    send_own(0)
    send_own(1)
    b_push = remote(b_all, bp_s, b_send, b_recv, place.peer)
    b_push.start()
    for k in range(WEIGHT_SLOTS - 1):
        fetch(jnp.int32(0), jnp.int32(k))
    gather.forward(0)
    send_own(2)
    gather.forward(1)
    send_own(3)
    b_push.wait_recv()
    for n in range(2 * n_sub):
        src = biases if n < n_sub else bp_s
        at = bias_at + (n % n_sub) * sub
        b_s[n // 2, :, (n % 2) * sub:(n % 2 + 1) * sub] = src[layer:layer + 1, at:at + sub].astype(F32)

    def chunk(c, carry):
        gather.finish(c)

        def up_step(k, inner):
            slot = landed(c, k)
            at = pl.multiple_of(k * WIDE, WIDE)
            for top in range(2):
                r0 = top * 2 * rows
                lifted = jnp.dot(x_s[c, r0:r0 + 2 * rows, :], w_s[slot], preferred_element_type=F32) + b_s[k]
                act_s[r0:r0 + 2 * rows, pl.ds(at, WIDE)] = gelu_tanh(lifted).astype(BF16)
            return inner

        lax.fori_loop(0, n_up, up_step, 0)

        @pl.when(c + 2 < chunks)
        def _():
            gather.forward(c + 2)

        @pl.when(c >= 2)
        def _():
            scatter.relay(c - 2)

        def down_step(k, inner):
            slot = landed(c, k)
            at = pl.multiple_of((k - n_up) * WIDE, WIDE)
            out_s[c, :, pl.ds(at, WIDE)] = jnp.dot(act_s[...], w_s[slot], preferred_element_type=F32).astype(BF16)
            return inner

        lax.fori_loop(n_up, n_tiles, down_step, 0)
        scatter.start(c)
        return carry

    lax.fori_loop(0, chunks, chunk, 0)
    scatter.close(mid_s, b_down[layer:layer + 1, :].astype(F32), h_out, h_sem, chunks, chunks - 2)
    for c in range(chunks):
        gather.drain(c)
    b_push.wait_send()


def run_mlp(layer, chunks, middle, norms, b_down, b_all, up, down, up_peer, down_peer):
    model = middle.shape[1]
    rows = middle.shape[0] // chunks
    ffn = up.shape[2]
    dims = (chunks, rows, model, ffn)
    flops = 2 * 4 * rows * chunks * model * ffn * 4
    return pl.pallas_call(
        functools.partial(mlp_kernel, layer, dims, b_all.shape[1] - ffn),
        out_shape=jax.ShapeDtypeStruct(middle.shape, BF16),
        in_specs=[ANY] + [VMEM] * 3 + [ANY] * 5,
        out_specs=ANY,
        scratch_shapes=[
            pltpu.VMEM((chunks, 4 * rows, model), BF16),
            pltpu.VMEM((chunks, 4 * rows, model), BF16),
            pltpu.VMEM((chunks, 3 * rows, model), BF16),
            pltpu.VMEM((4 * rows, 2 * ffn), BF16),
            pltpu.VMEM((WEIGHT_SLOTS, model, WIDE), BF16),
            pltpu.VMEM((chunks, rows, model), BF16),
            pltpu.VMEM((2 * ffn // WIDE, 1, WIDE), F32),
            pltpu.VMEM(b_all.shape, BF16),
            DMA((chunks, 4)),
            DMA((chunks, 4)),
            DMA((chunks, 6)),
            DMA((chunks, 6)),
            DMA((chunks,)),
            DMA((WEIGHT_SLOTS,)),
            DMA,
            DMA,
            DMA((chunks,)),
        ],
        compiler_params=pltpu.CompilerParams(vmem_limit_bytes=VMEM_LIMIT, collective_id=3 * layer + 2, has_side_effects=True),
        cost_estimate=pl.CostEstimate(flops=2 * flops, bytes_accessed=60_000_000, transcendentals=8 * rows * ffn),
        name=f"mlp_l{layer}",
    )(middle, norms, b_down, b_all, b_all, up, down, up_peer, down_peer)


def solution(mesh):
    row_spec = P('dp', 'tp', None)
    cache_spec = P(None, 'dp', None, 'tp', None)
    col_spec = P(None, None, 'tp')
    bias_spec = P(None, 'tp')
    in_specs = (row_spec, P('dp'), P('dp', None, None), P('dp', None, None), cache_spec, cache_spec, P('dp', None), P(), col_spec, bias_spec, col_spec, bias_spec, col_spec, bias_spec, P(None, 'tp', None), P(), col_spec, bias_spec, P(None, 'tp', None), P())
    out_specs = (row_spec, cache_spec, cache_spec, P('dp', None))

    def device_step(tokens, start_pos, cos_tab, sin_tab, key_cache, value_cache, slot_pos, norm_params, w_q, b_q, w_k, b_k, w_v, b_v, w_o, b_o, w_up, b_up, w_down, b_down):
        layers, _, window, _, hd = key_cache.shape
        cos, sin = cos_tab[0], sin_tab[0]
        kc = key_cache.reshape(layers, window, hd)
        vc = value_cache.reshape(layers, window, hd)
        b_all = jnp.concatenate([b_q, b_k, b_v, b_up], axis=1)
        hidden = tokens[0]
        fresh = []
        for layer in range(layers):
            q, kv_mine, kv_other, cache_mine, cache_peer, wo_peer, up_peer, down_peer = run_qkv(layer, CHUNKS, start_pos, hidden, norm_params, cos, sin, (w_q, w_k, w_v), b_all, (kc, vc, w_o, w_up, w_down))
            middle, kv_rolled = run_attn(layer, start_pos, q, kv_mine, kv_other, cache_mine, cache_peer, w_o, wo_peer, hidden, b_o)
            hidden = run_mlp(layer, CHUNKS, middle, norm_params, b_down, b_all, w_up, w_down, up_peer, down_peer)
            fresh.append(kv_rolled)
        key_out = jnp.stack([f[0] for f in fresh]).reshape(key_cache.shape)
        value_out = jnp.stack([f[1] for f in fresh]).reshape(value_cache.shape)
        first_slot = start_pos[0] % window
        pos_out = (start_pos[0] + (jnp.arange(window, dtype=jnp.int32) - first_slot) % window)[None]
        return hidden[None], key_out, value_out, pos_out

    return jax.shard_map(device_step, mesh=mesh, in_specs=in_specs, out_specs=out_specs, check_vma=False)
```

profile of v0, /device:TPU:0, one launch (start us, length us, event | category | flops | bytes accessed | tf_op | source)
XLA Modules:
  0.0 1118.3 jit_solution(4994115459430522499)
XLA Ops:
  1.3 0.7 constant_dynamic-update-slice_fusion.3
  2.0 0.7 constant_dynamic-update-slice_fusion.2
  2.7 0.7 constant_dynamic-update-slice_fusion.1
  3.3 0.7 constant_dynamic-update-slice_fusion.refs_7_.refs_8_.refs_3_.refs_4_
  4.0 0.0 copy-start.1
  4.1 0.6 copy-done.1
  4.6 139.3 %qkv_l0.1 = (bf16[4,2,4,2,128,256]{5,4,3,2,1,0:T(8,128)(2,1)}, bf16[2,4096,256]{2,1,0:T(8,128)(2,1)}, bf16[2,4096,256]{2,1,0:T(8,128)(2,1)}, bf16[2,4096,256]{2,...) custom-call(s32[1]{0:T(128)} %copy.29.scal, ...), custom_call_target="tpu_custom_call" | custom-call | flops 120259084288 | bytes 20000000 | tf_op jit(solution)/shard_map/qkv_l0/pallas_call | solution.py:326
  143.9 169.1 %attn_l0.1 = (bf16[512,3584]{1,0:T(8,128)(2,1)}, bf16[2,4096,256]{2,1,0:T(8,128)(2,1)}) custom-call(s32[1]{0:T(128)} %copy.29.scal, bf16[4,2,4,2,128,256]{5,4,3,2,1,0:T(8,128)(2,1)} %get-tuple-element.24.refs_0_, bf16[2,4096,256]{2,1,0:T(8,128)(2,1)} %get-tuple-element.25.refs_1_, bf16[2,4096,256]{2,1,0:T(8,128)(2,1)} %get-tuple-element.26.refs_2_, ...), custom_call_target="tpu_custom_call" | custom-call | flops 49392123904 | bytes 30000000 | tf_op jit(solution)/shard_map/attn_l0/pallas_call | solution.py:504
  313.1 243.7 %mlp_l0.1.refs_0_.refs_7_ = bf16[512,3584]{1,0:T(8,128)(2,1)} custom-call(bf16[512,3584]{1,0:T(8,128)(2,1)} %get-tuple-element.30.refs_0_, bf16[2,4,3584]{2,1,0:T(4,128)(2,1)} %refs_1_.7, bf16[2,3584]{1,0:T(2,128)(2,1)} %refs_2_.3, bf16[2,2816]{1,0:T(2,128)(2,1)} %copy-done.1, bf16[2,2816]{1,0:T(2,128)(2,1)} %copy-done.1, bf16[2,3584,1792]{2,1,0:T(8,128)(2,1)} %refs_5_.11, ...), custom_call_target="tpu_custom_call" | custom-call | flops 210453397504 | bytes 60000000 | tf_op jit(solution)/shard_map/mlp_l0/pallas_call | solution.py:657
  556.8 136.3 %qkv_l1.1 = (bf16[4,2,4,2,128,256]{5,4,3,2,1,0:T(8,128)(2,1)}, bf16[2,4096,256]{2,1,0:T(8,128)(2,1)}, bf16[2,4096,256]{2,1,0:T(8,128)(2,1)}, bf16[2,4096,256]{2,...) custom-call(s32[1]{0:T(128)} %copy.29.scal, ...), custom_call_target="tpu_custom_call" | custom-call | flops 120259084288 | bytes 20000000 | tf_op jit(solution)/shard_map/qkv_l1/pallas_call | solution.py:326
  693.1 169.4 %attn_l1.1 = (bf16[512,3584]{1,0:T(8,128)(2,1)}, bf16[2,4096,256]{2,1,0:T(8,128)(2,1)}) custom-call(s32[1]{0:T(128)} %copy.29.scal, bf16[4,2,4,2,128,256]{5,4,3,2,1,0:T(8,128)(2,1)} %get-tuple-element.33.refs_0_, bf16[2,4096,256]{2,1,0:T(8,128)(2,1)} %get-tuple-element.34.refs_1_, bf16[2,4096,256]{2,1,0:T(8,128)(2,1)} %get-tuple-element.35.refs_2_, ...), custom_call_target="tpu_custom_call" | custom-call | flops 49392123904 | bytes 30000000 | tf_op jit(solution)/shard_map/attn_l1/pallas_call | solution.py:504
  862.5 0.0 copy-start
  862.5 2.6 fusion.3
  865.2 0.8 copy-done
  866.0 0.3 fusion.2
  866.2 3.7 maximum_bitcast_fusion
  869.9 243.6 %mlp_l1.1 = bf16[512,3584]{1,0:T(8,128)(2,1)} custom-call(bf16[512,3584]{1,0:T(8,128)(2,1)} %get-tuple-element.39.refs_0_, bf16[2,4,3584]{2,1,0:T(4,128)(2,1)} %refs_1_.7, bf16[2,3584]{1,0:T(2,128)(2,1)} %refs_2_.3, bf16[2,2816]{1,0:T(2,128)(2,1)} %copy-done.1, bf16[2,2816]{1,0:T(2,128)(2,1)} %copy-done.1, bf16[2,3584,1792]{2,1,0:T(8,128)(2,1)} %refs_5_.11, ...), custom_call_target="tpu_custom_call" | custom-call | flops 210453397504 | bytes 60000000 | tf_op jit(solution)/shard_map/mlp_l1/pallas_call | solution.py:657
  1113.6 0.7 fusion
  1114.2 4.1 copy.30
Async XLA Ops:
  4.0 0.6 copy-start.1
  862.5 3.5 copy-start
where the time goes:
time: 1120 us
  Pallas kernels  1100 us (98%)
    pallas_call x2, Pallas kernels, run_mlp(): pl.pallas_call(functools.partial(mlp_kernel, layer, dims, b_all.shape[1]...  487 us
    pallas_call x2, Pallas kernels, run_attn(): pl.pallas_call(functools.partial(attn_kernel, layer, dims), out_shape=(ja...  339 us
    pallas_call x2, Pallas kernels, run_qkv(): pl.pallas_call(functools.partial(qkv_kernel, layer, dims), out_shape=tupl...  276 us

commit v1 on v0

v1 whole, which is shorter than its diff:
```python
import functools

import jax
import jax.numpy as jnp
from jax import lax
from jax.experimental import pallas as pl
from jax.experimental.pallas import tpu as pltpu
from jax.sharding import PartitionSpec as P

NORM_EPS = 1e-5
LOG2E = 1.4426950408889634
CHUNKS = 4
KEY_TILE = 512
LANES = 128
WIDE = 512
ROW_BLOCK = 16
WEIGHT_SLOTS = 3
ROLL_ROWS = 256
EARLY = 2
LOWEST = -3.3e38
VMEM_LIMIT = 62 * 1024 * 1024
BF16 = jnp.bfloat16
F32 = jnp.float32
MESH = pl.DeviceIdType.MESH

ANY = pl.BlockSpec(memory_space=pl.ANY)
SMEM = pl.BlockSpec(memory_space=pltpu.SMEM)
VMEM = pl.BlockSpec(memory_space=pltpu.VMEM)
DMA = pltpu.SemaphoreType.DMA


def gelu_tanh(x):
    inner = 0.7978845608028654 * (x + 0.044715 * (x * x * x))
    return 0.5 * x * (1.0 + jnp.tanh(inner))


def normalized(values, gain, shift):
    centered = values - jnp.mean(values, axis=-1, keepdims=True)
    variance = jnp.mean(centered * centered, axis=-1, keepdims=True)
    return (centered * lax.rsqrt(variance + NORM_EPS) * gain + shift).astype(BF16)


def rotate(planes, dst, window, shift, first, last):
    def tile(n, carry):
        at = pl.multiple_of(n * ROLL_ROWS, ROLL_ROWS)
        want = lax.broadcasted_iota(jnp.int32, (ROLL_ROWS, 1), 0) + (n * ROLL_ROWS + shift)
        want = jnp.where(want >= window, want - window, want)
        pick = jnp.where(lax.broadcasted_iota(jnp.int32, (1, window), 1) == want, 1.0, 0.0).astype(BF16)
        for k in range(2):
            dst[k, pl.ds(at, ROLL_ROWS), :] = jnp.dot(pick, planes(k), preferred_element_type=F32).astype(BF16)
        return carry

    lax.fori_loop(first, last, tile, 0)


def reset_state(st_s, w):
    for g in range(2):
        st_s[w, g, :, 0:LANES] = jnp.full((st_s.shape[2], LANES), LOWEST, F32)
        st_s[w, g, :, LANES:] = jnp.zeros((st_s.shape[2], st_s.shape[3] - LANES), F32)


def flash_step(st_s, w, s_s, scale, mask, values, next_scores):
    for g in range(2):
        s = jnp.where(mask, s_s[g] * scale, -jnp.inf)
        s_next = next_scores(g)
        m_prev = st_s[w, g, :, 0:LANES]
        m_next = jnp.maximum(m_prev, jnp.max(s, axis=1, keepdims=True))
        e = jnp.exp2(s - jnp.concatenate([m_next] * (s.shape[1] // LANES), axis=1))
        alpha = jnp.exp2(m_prev - m_next)
        total = st_s[w, g, :, LANES:2 * LANES] * alpha
        for k in range(s.shape[1] // LANES):
            total = total + e[:, k * LANES:(k + 1) * LANES]
        st_s[w, g, :, LANES:2 * LANES] = total
        st_s[w, g, :, 0:LANES] = m_next
        mixed = jnp.dot(e.astype(BF16), values(g), preferred_element_type=F32)
        st_s[w, g, :, 2 * LANES:] = st_s[w, g, :, 2 * LANES:] * jnp.concatenate([alpha] * (mixed.shape[1] // LANES), axis=1) + mixed
        s_s[g] = s_next


def score_tile(queries, keys):
    return lax.dot_general(queries, keys, (((1,), (1,)), ((), ())), preferred_element_type=F32)


class Place:
    def __init__(self):
        me = lax.axis_index('tp')
        self.core = lax.rem(me, 2)
        self.xb = lax.rem(lax.div(me, 2), 2)
        self.yb = lax.div(me, 4)
        self.peer = me + 1 - 2 * self.core
        self.x = me + 2 - 4 * self.xb
        self.y = me + 4 - 8 * self.yb

    def member(self, i):
        xb = self.xb + lax.rem(i, 2) * (1 - 2 * self.xb)
        yb = self.yb + lax.div(i, 2) * (1 - 2 * self.yb)
        return yb * 2 + xb

    def barrier(self, others):
        sem = pltpu.get_barrier_semaphore()
        for other in others:
            pl.semaphore_signal(sem, inc=1, device_id={'tp': other}, device_id_type=MESH)
        pl.semaphore_wait(sem, len(others))


def remote(src, dst, send_sem, recv_sem, other):
    return pltpu.make_async_remote_copy(src_ref=src, dst_ref=dst, send_sem=send_sem, recv_sem=recv_sem, device_id={'tp': other}, device_id_type=MESH)


class Gather:
    def __init__(self, place, x_s, send, recv, rows):
        self.place, self.x_s, self.send, self.recv, self.rows = place, x_s, send, recv, rows

    def copy(self, c, kind):
        r, h = self.rows, self.rows // 2
        src, dst, size, other = ((0, r, r, self.place.x), (0, 2 * r, r, self.place.y), (r, 3 * r, h, self.place.y), (2 * r + h, 3 * r + h, h, self.place.x))[kind]
        return remote(self.x_s.at[c, pl.ds(src, size)], self.x_s.at[c, pl.ds(dst, size)], self.send.at[c, kind], self.recv.at[c, kind], other)

    def start(self, c):
        self.copy(c, 0).start()
        self.copy(c, 1).start()

    def forward(self, c):
        self.copy(c, 0).wait_recv()
        self.copy(c, 2).start()
        self.copy(c, 1).wait_recv()
        self.copy(c, 3).start()

    def finish(self, c):
        self.copy(c, 2).wait_recv()
        self.copy(c, 3).wait_recv()

    def drain(self, c):
        for kind in range(4):
            self.copy(c, kind).wait_send()


class Scatter:
    def __init__(self, place, out_s, land_s, send, recv, rows):
        self.place, self.out_s, self.land_s, self.send, self.recv, self.rows = place, out_s, land_s, send, recv, rows

    def copy(self, c, kind):
        r, h = self.rows, self.rows // 2
        x, y = self.place.x, self.place.y
        src, dst, other = ((3 * r, 2 * r, x), (3 * r + h, 2 * r + h, y), (r, 0, x), (2 * r + h, r + h, y), (r + h, h, x), (2 * r, r, y))[kind]
        return remote(self.out_s.at[c, pl.ds(src, h)], self.land_s.at[c, pl.ds(dst, h)], self.send.at[c, kind], self.recv.at[c, kind], other)

    def start(self, c):
        for kind in range(4):
            self.copy(c, kind).start()

    def add(self, c, kind, src, dst):
        self.copy(c, kind).wait_recv()

        def block(n, carry):
            at = pl.multiple_of(n * ROW_BLOCK, ROW_BLOCK)
            mine = self.out_s[c, pl.ds(dst + at, ROW_BLOCK), :].astype(F32)
            came = self.land_s[c, pl.ds(src + at, ROW_BLOCK), :].astype(F32)
            self.out_s[c, pl.ds(dst + at, ROW_BLOCK), :] = (mine + came).astype(BF16)
            return carry

        lax.fori_loop(0, self.rows // 2 // ROW_BLOCK, block, 0)

    def relay(self, c):
        r, h = self.rows, self.rows // 2
        self.add(c, 0, 2 * r, 2 * r)
        self.copy(c, 5).start()
        self.add(c, 1, 2 * r + h, r + h)
        self.copy(c, 4).start()

    def finish(self, c):
        for kind in range(2, 6):
            self.copy(c, kind).wait_recv()

    def close(self, mid_s, bias, out, o_sem, chunks, first_open):
        rows = self.rows

        def o_copy(c):
            return pltpu.make_async_copy(mid_s.at[c], out.at[pl.ds(pl.multiple_of(c * rows, rows), rows)], o_sem.at[c])

        def one(c, carry):
            @pl.when(c + first_open < chunks)
            def _():
                self.relay(c + first_open)

            self.finish(c)

            def block(n, inner):
                at = pl.multiple_of(n * ROW_BLOCK, ROW_BLOCK)
                total = self.out_s[c, pl.ds(at, ROW_BLOCK), :].astype(F32) + self.land_s[c, pl.ds(at, ROW_BLOCK), :].astype(F32) + self.land_s[c, pl.ds(rows + at, ROW_BLOCK), :].astype(F32)
                mid_s[c, pl.ds(at, ROW_BLOCK), :] = (mid_s[c, pl.ds(at, ROW_BLOCK), :].astype(F32) + total + bias).astype(BF16)
                return inner

            lax.fori_loop(0, rows // ROW_BLOCK, block, 0)
            o_copy(c).start()
            return carry

        lax.fori_loop(0, chunks, one, 0)

        def settle(c, carry):
            o_copy(c).wait()
            for kind in range(6):
                self.copy(c, kind).wait_send()
            return carry

        lax.fori_loop(0, chunks, settle, 0)


def qkv_kernel(layer, dims, scal, *refs):
    chunks, rows, model, hd, window = dims
    hidden, norms, cos, sin, wq, wk, wv = refs[:7]
    biases, b_push = refs[7:10], refs[10:13]
    kc, vc, wo, w_up, w_down = refs[13:18]
    q_out, kv_mine, kv_other, cache_mine, cache_peer, wo_peer, up_peer, down_peer, state = refs[18:27]
    x_s, h_s, t_s, w_s, b_s, bq_s, bk_s, bv_s, oq_s, okv_s, old_s, oldp_s, st_s, s_s = refs[27:41]
    ag_send, ag_recv, h_sem, t_sem, w_sem, wr_send, wr_recv, p_send, p_recv, q_sem, kv_sem, kr_send, kr_recv, raw_sem, old_sem, st_sem = refs[41:]
    place = Place()
    block = rows * chunks
    tall = 2 * rows
    tile = KEY_TILE
    tiles = window // tile
    scale = LOG2E * hd ** -0.5
    floor = window - 1 - scal[0]
    loads = [pltpu.make_async_copy(hidden.at[pl.ds(c * rows, rows)], h_s.at[c], h_sem.at[c]) for c in range(chunks)]
    for copy in loads:
        copy.start()
    for k, cache in enumerate((kc, vc)):
        pltpu.make_async_copy(cache.at[layer], okv_s.at[pl.ds(k * window, window)], raw_sem).start()
    place.barrier((place.x, place.y, place.peer))
    gather = Gather(place, x_s, ag_send, ag_recv, rows)
    parts = ((wq.at[layer], 0, 0, 2 * hd), (wk.at[layer], 1, 0, hd), (wv.at[layer], 1, hd, hd))
    w_local = [pltpu.make_async_copy(src, w_s.at[t, :, pl.ds(at, n)], w_sem.at[k]) for k, (src, t, at, n) in enumerate(parts)]
    w_remote = [remote(src, w_s.at[2 + t, :, pl.ds(at, n)], wr_send.at[k], wr_recv.at[k], place.peer) for k, (src, t, at, n) in enumerate(parts)]
    b_remote = [remote(src, dst, wr_send.at[3 + k], wr_recv.at[3 + k], place.peer) for k, (src, dst) in enumerate(zip(b_push, (bq_s, bk_s, bv_s)))]
    landing = (wo_peer, up_peer, down_peer)
    pushes = [remote(src.at[layer], dst, p_send.at[k], p_recv.at[k], place.peer) for k, (src, dst) in enumerate(zip((wo, w_up, w_down), landing))]
    old_push = remote(old_s, oldp_s, p_send.at[3], p_recv.at[3], place.peer)
    old_store = [pltpu.make_async_copy(src, dst, old_sem.at[k]) for k, (src, dst) in enumerate(((old_s, cache_mine), (oldp_s, cache_peer)))]
    gain = norms[layer, 0:1, :].astype(F32)
    shift = norms[layer, 1:2, :].astype(F32)

    def send_own(c):
        loads[c].wait()

        def norm_block(n, carry):
            at = pl.multiple_of(n * ROW_BLOCK, ROW_BLOCK)
            x_s[c, pl.ds(at, ROW_BLOCK), :] = normalized(h_s[c, pl.ds(at, ROW_BLOCK), :].astype(F32), gain, shift)
            return carry

        lax.fori_loop(0, rows // ROW_BLOCK, norm_block, 0)
        gather.start(c)

    def chunk_pos(c, i):
        return pl.multiple_of((place.member(i) * 2 + place.core) * block + c * rows, rows)

    def kv_row(c, kv, g):
        return ((c * 2 + kv) * 2 + g) * 4 * rows

    send_own(0)
    send_own(1)
    for copy in b_remote + w_remote + w_local + pushes:
        copy.start()
    for c in range(chunks):
        for i in range(4):
            for k, tab in enumerate((cos, sin)):
                pltpu.make_async_copy(tab.at[pl.ds(chunk_pos(c, i), rows)], t_s.at[c, k, pl.ds(i * rows, rows)], t_sem.at[c]).start()
    raw = okv_s.at[pl.ds(0, 2 * window)]
    pltpu.make_async_copy(raw, raw, raw_sem).wait()
    first_slot = lax.rem(scal[0], window)
    roll_tiles = window // ROLL_ROWS

    def raw_plane(k):
        return okv_s[k * window:(k + 1) * window, :]

    rotate(raw_plane, old_s, window, first_slot, 0, roll_tiles // 3)
    gather.forward(0)
    send_own(2)
    rotate(raw_plane, old_s, window, first_slot, roll_tiles // 3, roll_tiles)
    old_push.start()
    old_store[0].start()
    gather.forward(1)
    for copy in b_remote:
        copy.wait_recv()
    for g, (bq, bk, bv) in enumerate((biases, (bq_s, bk_s, bv_s))):
        b_s[2 * g] = bq[layer:layer + 1, :].astype(F32)
        b_s[2 * g + 1, :, 0:hd] = bk[layer:layer + 1, :].astype(F32)
        b_s[2 * g + 1, :, hd:] = bv[layer:layer + 1, :].astype(F32)

    def project(c, i0, count):
        r0, n = i0 * rows, count * rows

        def rope(u):
            turned = jnp.concatenate([-u[:, hd // 2:], u[:, :hd // 2]], axis=1)
            return (u * t_s[c, 0, r0:r0 + n, :] + turned * t_s[c, 1, r0:r0 + n, :]).astype(BF16)

        def side(g, carry):
            u = jnp.dot(x_s[c, r0:r0 + n, :], w_s[2 * g], preferred_element_type=F32) + b_s[2 * g]
            for h in range(2):
                oq_s[c, g, i0:i0 + count, h] = rope(u[:, h * hd:(h + 1) * hd]).reshape(count, rows, hd)
            u = jnp.dot(x_s[c, r0:r0 + n, :], w_s[2 * g + 1], preferred_element_type=F32) + b_s[2 * g + 1]
            okv_s[pl.ds(pl.multiple_of(kv_row(c, 0, g) + r0, rows), n), :] = rope(u[:, :hd])
            okv_s[pl.ds(pl.multiple_of(kv_row(c, 1, g) + r0, rows), n), :] = u[:, hd:].astype(BF16)
            return carry

        lax.fori_loop(0, 2, side, 0)

    def q_copy(c):
        return pltpu.make_async_copy(oq_s.at[c], q_out.at[c], q_sem.at[c])

    def kv_copies(c):
        planes = (kv_mine, kv_other)
        made = []
        for kv in range(2):
            for g in range(2):
                for i in range(4):
                    src = okv_s.at[pl.ds(pl.multiple_of(kv_row(c, kv, g) + i * rows, rows), rows)]
                    at = pl.ds(chunk_pos(c, i), rows)
                    made.append(pltpu.make_async_copy(src, planes[g].at[kv, at], kv_sem.at[c]))
                    made.append(remote(src, planes[1 - g].at[kv, at], kr_send.at[c], kr_recv.at[c], place.peer))
        return made

    def old_tile(g, kv, at):
        return (old_s, oldp_s)[g][kv, pl.ds(at, tile), :]

    def queries(c, i, g):
        return oq_s[c, g, i].reshape(tall, hd)

    def state_copy(b):
        return pltpu.make_async_copy(st_s.at[lax.rem(b, 2)], state.at[b], st_sem.at[lax.rem(b, 2)])

    def start_old(c, i):
        at = pl.multiple_of(lax.div(chunk_pos(c, i), tile) * tile, tile)
        for g in range(2):
            s_s[g] = score_tile(queries(c, i, g), old_tile(g, 0, at))

    def attend_old(c, i):
        b = c * 4 + i
        w = lax.rem(b, 2)
        j0 = chunk_pos(c, i)
        diag = lax.div(j0, tile)
        i_next = jnp.minimum(i + 1, 3)
        diag_next = lax.div(chunk_pos(c, i_next), tile)

        @pl.when(b >= 2)
        def _():
            state_copy(b - 2).wait()

        reset_state(st_s, w)

        def step(t, by_row):
            at = pl.multiple_of(t * tile, tile)
            last = t + 1 == tiles
            n_at = pl.multiple_of(jnp.where(last, diag_next, t + 1) * tile, tile)
            n_i = jnp.where(last, i_next, i)
            age = lax.broadcasted_iota(jnp.int32, (1, tile), 1) + at
            if by_row:
                row = lax.rem(lax.broadcasted_iota(jnp.int32, (tall, 1), 0), rows) + j0
                mask = age > jnp.maximum(row, floor)
            else:
                mask = age > floor
            flash_step(st_s, w, s_s, scale, mask, lambda g: old_tile(g, 1, at), lambda g: score_tile(queries(c, n_i, g), old_tile(g, 0, n_at)))

        step(diag, True)

        def younger(t, carry):
            @pl.when(t > diag)
            def _():
                step(t, False)

            return carry

        lax.fori_loop(1, tiles, younger, 0)
        state_copy(b).start()

    def chunk(c, carry):
        pltpu.make_async_copy(t_s.at[c], t_s.at[c], t_sem.at[c]).wait()

        @pl.when(c == 0)
        def _():
            for copy in w_local:
                copy.wait()
            for copy in w_remote:
                copy.wait_recv()

        project(c, 0, 3)
        gather.finish(c)
        project(c, 3, 1)
        q_copy(c).start()
        for copy in kv_copies(c):
            copy.start()

        @pl.when(c == 0)
        def _():
            old_push.wait_recv()
            old_store[1].start()

        @pl.when(lax.rem(c, 2) == 0)
        def _():
            early = lax.div(c, 2)
            start_old(early, 0)

            def one(i, inner):
                @pl.when(jnp.logical_and(c == 2, i == 3))
                def _():
                    gather.forward(3)

                attend_old(early, i)
                return inner

            lax.fori_loop(0, 4, one, 0)

        @pl.when(c == 0)
        def _():
            gather.forward(2)
            send_own(3)

        return carry

    lax.fori_loop(0, chunks, chunk, 0)
    for copy in w_remote + b_remote:
        copy.wait_send()

    def settle(c, carry):
        q_copy(c).wait()
        whole = okv_s.at[pl.ds(pl.multiple_of(kv_row(c, 0, 0), rows), 16 * rows)]
        pltpu.make_async_copy(whole, whole, kv_sem.at[c]).wait()
        remote(whole, whole, kr_send.at[c], kr_recv.at[c], place.peer).wait_send()
        remote(whole, whole, kr_send.at[c], kr_recv.at[c], place.peer).wait_recv()
        gather.drain(c)
        return carry

    lax.fori_loop(0, chunks, settle, 0)
    for copy in pushes:
        copy.wait_send()
        copy.wait_recv()
    old_push.wait_send()
    for copy in old_store:
        copy.wait()
    for b in (4 * EARLY - 2, 4 * EARLY - 1):
        state_copy(b).wait()


def run_qkv(layer, chunks, scal, hidden, norms, cos, sin, weights, biases, caches, w_o, w_up, w_down):
    model = hidden.shape[1]
    rows = hidden.shape[0] // chunks
    hd = cos.shape[1]
    window = cos.shape[0]
    dims = (chunks, rows, model, hd, window)
    flops = 2 * 4 * rows * chunks * model * 8 * hd
    shapes = [(chunks, 2, 4, 2, rows, hd)] + [(2, window, hd)] * 4 + [w.shape[1:] for w in (w_o, w_up, w_down)]
    state = (4 * EARLY, 2, 2 * rows, 2 * LANES + hd)
    return pl.pallas_call(
        functools.partial(qkv_kernel, layer, dims),
        out_shape=tuple(jax.ShapeDtypeStruct(s, BF16) for s in shapes) + (jax.ShapeDtypeStruct(state, F32),),
        in_specs=[SMEM, ANY, VMEM] + [ANY] * 5 + [VMEM] * 3 + [ANY] * 8,
        out_specs=(ANY,) * (len(shapes) + 1),
        scratch_shapes=[
            pltpu.VMEM((chunks, 4 * rows, model), BF16),
            pltpu.VMEM((chunks, rows, model), BF16),
            pltpu.VMEM((chunks, 2, 4 * rows, hd), F32),
            pltpu.VMEM((4, model, 2 * hd), BF16),
            pltpu.VMEM((4, 1, 2 * hd), F32),
        ] + [pltpu.VMEM(b.shape, BF16) for b in biases] + [
            pltpu.VMEM((chunks, 2, 4, 2, rows, hd), BF16),
            pltpu.VMEM((chunks * 16 * rows, hd), BF16),
            pltpu.VMEM((2, window, hd), BF16),
            pltpu.VMEM((2, window, hd), BF16),
            pltpu.VMEM((2,) + state[1:], F32),
            pltpu.VMEM((2, 2 * rows, KEY_TILE), F32),
            DMA((chunks, 4)),
            DMA((chunks, 4)),
            DMA((chunks,)),
            DMA((chunks,)),
            DMA((3,)),
            DMA((6,)),
            DMA((6,)),
            DMA((4,)),
            DMA((4,)),
            DMA((chunks,)),
            DMA((chunks,)),
            DMA((chunks,)),
            DMA((chunks,)),
            DMA,
            DMA((2,)),
            DMA((2,)),
        ],
        compiler_params=pltpu.CompilerParams(vmem_limit_bytes=VMEM_LIMIT, collective_id=3 * layer, has_side_effects=True),
        cost_estimate=pl.CostEstimate(flops=4 * flops, bytes_accessed=20_000_000, transcendentals=0),
        name=f"qkv_l{layer}",
    )(scal, hidden, norms, cos, sin, *weights, *biases, *biases, *caches, w_o, w_up, w_down)


def attn_kernel(layer, dims, scal, *refs):
    chunks, rows, model, hd, window = dims
    q, kv_mine, kv_other, cache_mine, cache_peer, state, wo, wo_peer, hidden, b_o = refs[:10]
    mid_out, kv_rolled = refs[10:12]
    kv_s, q_s, s_s, mix_s, wo_s, out_s, land_s, mid_s, st_s, rs_send, rs_recv, new_sem, old_sem, q_sem, w_sem, h_sem, st_sem, o_sem, f_sem = refs[12:]
    place = Place()
    start_pos = scal[0]
    block = rows * chunks
    tall = 2 * rows
    tile = KEY_TILE
    tiles = window // tile
    scale = LOG2E * hd ** -0.5
    q_load = pltpu.make_async_copy(q, q_s, q_sem)
    q_load.start()
    new = kv_s.at[:, pl.ds(2, 2)]
    old = kv_s.at[:, pl.ds(0, 2)]
    for g, src in enumerate((kv_mine, kv_other)):
        pltpu.make_async_copy(src, kv_s.at[g, pl.ds(2, 2)], new_sem).start()

    def pick(k):
        return jnp.where(k == 0, 3, jnp.where(k == 3, 0, k))

    def state_copy(b):
        return pltpu.make_async_copy(state.at[lax.div(b, 4) * 4 + pick(lax.rem(b, 4))], st_s.at[lax.rem(b, 2)], st_sem.at[lax.rem(b, 2)])

    for b in range(2):
        state_copy(jnp.int32(b)).start()
    pltpu.make_async_copy(wo.at[layer], wo_s.at[pl.ds(0, 2 * hd)], w_sem).start()
    pltpu.make_async_copy(wo_peer, wo_s.at[pl.ds(2 * hd, 2 * hd)], w_sem).start()
    for g, src in enumerate((cache_mine, cache_peer)):
        pltpu.make_async_copy(src, kv_s.at[g, pl.ds(0, 2)], old_sem).start()
    for c in range(chunks):
        pltpu.make_async_copy(hidden.at[pl.ds(c * rows, rows)], mid_s.at[c], h_sem).start()
    place.barrier((place.x, place.y))
    scatter = Scatter(place, out_s, land_s, rs_send, rs_recv, rows)
    first_slot = lax.rem(start_pos, window)
    floor = window - 1 - start_pos

    def first_row(c, i):
        return (place.member(i) * 2 + place.core) * block + c * rows

    def tile_at(diag, n):
        is_new = jnp.logical_or(n == 0, jnp.logical_and(n >= 2, n - 2 < diag))
        t = jnp.where(n < 2, diag, jnp.where(is_new, n - 2, n - 1))
        return jnp.where(is_new, 2, 0), pl.multiple_of(t * tile, tile), is_new

    def scores(c, i, g, which, at):
        return score_tile(q_s[c, g, i].reshape(tall, hd), kv_s[g, which, pl.ds(at, tile), :])

    q_load.wait()
    pltpu.make_async_copy(new, new, new_sem).wait()
    for g in range(2):
        s_s[g] = scores(0, 3, g, 2, pl.multiple_of(lax.div(first_row(0, 3), tile) * tile, tile))

    def attend(c, k):
        i = pick(k)
        b = c * 4 + k
        w = lax.rem(b, 2)
        whole = c >= EARLY
        j0 = first_row(c, i)
        diag = lax.div(j0, tile)
        count = jnp.where(whole, tiles + 1, diag + 2)
        end = k == 3
        c_next = jnp.minimum(jnp.where(end, c + 1, c), chunks - 1)
        i_next = pick(jnp.where(end, 0, k + 1))
        next_at = lax.div(first_row(c_next, i_next), tile) * tile

        @pl.when(whole)
        def _():
            reset_state(st_s, w)

        @pl.when(jnp.logical_not(whole))
        def _():
            state_copy(b).wait()

        def step(n):
            which, at, is_new = tile_at(diag, n)
            following = jnp.where(jnp.logical_and(n == 0, jnp.logical_not(whole)), 2, n + 1)
            last = following == count
            nw, nat, _ = tile_at(diag, following)
            nw = jnp.where(last, 2, nw)
            nat = pl.multiple_of(jnp.where(last, next_at, nat), tile)
            nc = jnp.where(last, c_next, c)
            ni = jnp.where(last, i_next, i)
            col = lax.broadcasted_iota(jnp.int32, (1, tile), 1) + at
            row = lax.rem(lax.broadcasted_iota(jnp.int32, (tall, 1), 0), rows) + j0
            if not isinstance(n, int):
                mask = col > jnp.where(is_new, -1, floor)
            elif n == 0:
                mask = col <= row
            else:
                mask = col > jnp.maximum(row, floor)
            flash_step(st_s, w, s_s, scale, mask, lambda g: kv_s[g, which + 1, pl.ds(at, tile), :], lambda g: scores(nc, ni, g, nw, nat))

        step(0)

        @pl.when(whole)
        def _():
            step(1)

        def further(n, carry):
            @pl.when(n < count)
            def _():
                step(n)

            return carry

        lax.fori_loop(2, tiles + 1, further, 0)
        for g in range(2):
            total = jnp.sum(st_s[w, g, :, LANES:2 * LANES], axis=1, keepdims=True)
            out = (st_s[w, g, :, 2 * LANES:] / total).astype(BF16)
            for h in range(2):
                mix_s[:, (2 * g + h) * hd:(2 * g + h + 1) * hd] = out[h * rows:(h + 1) * rows]

        @pl.when(b + 2 < 4 * EARLY)
        def _():
            state_copy(b + 2).start()

        @pl.when(b == 0)
        def _():
            pltpu.make_async_copy(wo_s, wo_s, w_sem).wait()

        r0 = pl.multiple_of(i * rows, rows)
        for n in range(model // WIDE):
            out_s[c, pl.ds(r0, rows), n * WIDE:(n + 1) * WIDE] = jnp.dot(mix_s[...], wo_s[:, n * WIDE:(n + 1) * WIDE], preferred_element_type=F32).astype(BF16)

        @pl.when(k == 0)
        def _():
            scatter.copy(c, 0).start()
            scatter.copy(c, 1).start()

        @pl.when(k == 1)
        def _():
            scatter.copy(c, 2).start()

        @pl.when(k == 2)
        def _():
            scatter.copy(c, 3).start()

    def chunk(c, carry):
        @pl.when(c == EARLY)
        def _():
            pltpu.make_async_copy(old, old, old_sem).wait()

        def one(k, inner):
            attend(c, k)

            @pl.when(jnp.logical_and(k == 1, c >= 1))
            def _():
                scatter.relay(c - 1)

            return inner

        lax.fori_loop(0, 4, one, 0)
        return carry

    lax.fori_loop(0, chunks, chunk, 0)
    pltpu.make_async_copy(mid_s, mid_s, h_sem).wait()
    rolled = kv_s.at[1, pl.ds(0, 2)]
    roll_tiles = window // ROLL_ROWS

    def new_plane(k):
        return kv_s[0, 2 + k]

    rotate(new_plane, rolled, window, window - first_slot, 0, roll_tiles // 2)
    scatter.relay(chunks - 1)
    rotate(new_plane, rolled, window, window - first_slot, roll_tiles // 2, roll_tiles)
    roll_store = pltpu.make_async_copy(rolled, kv_rolled, f_sem)
    roll_store.start()
    scatter.close(mid_s, b_o[layer:layer + 1, :].astype(F32), mid_out, o_sem, chunks, chunks)
    roll_store.wait()


def run_attn(layer, scal, q, kv_mine, kv_other, cache_mine, cache_peer, state, wo, wo_peer, hidden, b_o):
    chunks, rows, hd = q.shape[0], q.shape[-2], q.shape[-1]
    model = hidden.shape[1]
    window = kv_mine.shape[1]
    dims = (chunks, rows, model, hd, window)
    flops = 4 * 4 * rows * chunks * 4 * window * hd + 2 * 4 * rows * chunks * 4 * hd * model
    return pl.pallas_call(
        functools.partial(attn_kernel, layer, dims),
        out_shape=(jax.ShapeDtypeStruct(hidden.shape, BF16), jax.ShapeDtypeStruct((2, window, hd), BF16)),
        in_specs=[SMEM] + [ANY] * 9 + [VMEM],
        out_specs=(ANY, ANY),
        scratch_shapes=[
            pltpu.VMEM((2, 4, window, hd), BF16),
            pltpu.VMEM((chunks, 2, 4, 2, rows, hd), BF16),
            pltpu.VMEM((2, 2 * rows, KEY_TILE), F32),
            pltpu.VMEM((rows, 4 * hd), BF16),
            pltpu.VMEM((4 * hd, model), BF16),
            pltpu.VMEM((chunks, 4 * rows, model), BF16),
            pltpu.VMEM((chunks, 3 * rows, model), BF16),
            pltpu.VMEM((chunks, rows, model), BF16),
            pltpu.VMEM((2,) + state.shape[1:], F32),
            DMA((chunks, 6)),
            DMA((chunks, 6)),
            DMA,
            DMA,
            DMA,
            DMA,
            DMA,
            DMA((2,)),
            DMA((chunks,)),
            DMA,
        ],
        compiler_params=pltpu.CompilerParams(vmem_limit_bytes=VMEM_LIMIT, collective_id=3 * layer + 1, has_side_effects=True),
        cost_estimate=pl.CostEstimate(flops=flops, bytes_accessed=30_000_000, transcendentals=16 * rows * chunks * window),
        name=f"attn_l{layer}",
    )(scal, q, kv_mine, kv_other, cache_mine, cache_peer, state, wo, wo_peer, hidden, b_o)


def mlp_kernel(layer, dims, *refs):
    chunks, rows, model, ffn = dims
    middle, norms, b_down, biases, b_up, up, down, up_peer, down_peer = refs[:9]
    h_out = refs[9]
    x_s, out_s, land_s, act_s, w_s, mid_s, b_s, bp_s, ag_send, ag_recv, rs_send, rs_recv, m_sem, w_sem, b_send, b_recv, h_sem = refs[10:]
    place = Place()
    n_up = 2 * ffn // WIDE
    n_tiles = n_up + model // WIDE
    sub = WIDE // 2
    n_sub = ffn // sub
    ups = (up.at[layer], up_peer)
    downs = (down.at[layer], down_peer)
    loads = [pltpu.make_async_copy(middle.at[pl.ds(c * rows, rows)], mid_s.at[c], m_sem.at[c]) for c in range(chunks)]
    for copy in loads:
        copy.start()
    place.barrier((place.x, place.y, place.peer))
    gather = Gather(place, x_s, ag_send, ag_recv, rows)
    scatter = Scatter(place, out_s, land_s, rs_send, rs_recv, rows)
    gain = norms[layer, 2:3, :].astype(F32)
    shift = norms[layer, 3:4, :].astype(F32)

    def fetch(c, k):
        over = k >= n_tiles
        k = jnp.where(over, k - n_tiles, k)
        c = jnp.where(over, c + 1, c)
        slot = lax.rem(c * n_tiles + k, WEIGHT_SLOTS)

        @pl.when(c < chunks)
        def _():
            for part in range(2):
                n = 2 * k + part
                for side in range(2):
                    @pl.when(jnp.logical_and(n >= side * n_sub, n < (side + 1) * n_sub))
                    def _():
                        at = pl.multiple_of((n - side * n_sub) * sub, sub)
                        pltpu.make_async_copy(ups[side].at[:, pl.ds(at, sub)], w_s.at[slot, :, pl.ds(part * sub, sub)], w_sem.at[slot]).start()

            @pl.when(k >= n_up)
            def _():
                at = pl.multiple_of((k - n_up) * WIDE, WIDE)
                for side in range(2):
                    pltpu.make_async_copy(downs[side].at[:, pl.ds(at, WIDE)], w_s.at[slot, pl.ds(side * ffn, ffn)], w_sem.at[slot]).start()

    def landed(c, k):
        slot = lax.rem(c * n_tiles + k, WEIGHT_SLOTS)
        pltpu.make_async_copy(w_s.at[slot], w_s.at[slot], w_sem.at[slot]).wait()
        fetch(c, k + WEIGHT_SLOTS - 1)
        return slot

    def send_own(c):
        loads[c].wait()

        def norm_block(n, carry):
            at = pl.multiple_of(n * ROW_BLOCK, ROW_BLOCK)
            x_s[c, pl.ds(at, ROW_BLOCK), :] = normalized(mid_s[c, pl.ds(at, ROW_BLOCK), :].astype(F32), gain, shift)
            return carry

        lax.fori_loop(0, rows // ROW_BLOCK, norm_block, 0)
        gather.start(c)

    send_own(0)
    send_own(1)
    b_push = remote(b_up, bp_s, b_send, b_recv, place.peer)
    b_push.start()
    for k in range(WEIGHT_SLOTS - 1):
        fetch(jnp.int32(0), jnp.int32(k))
    gather.forward(0)
    send_own(2)
    gather.forward(1)
    send_own(3)
    b_push.wait_recv()
    for n in range(2 * n_sub):
        src = biases if n < n_sub else bp_s
        at = (n % n_sub) * sub
        b_s[n // 2, :, (n % 2) * sub:(n % 2 + 1) * sub] = src[layer:layer + 1, at:at + sub].astype(F32)

    def chunk(c, carry):
        gather.finish(c)

        def up_step(k, inner):
            slot = landed(c, k)
            at = pl.multiple_of(k * WIDE, WIDE)
            for top in range(2):
                r0 = top * 2 * rows
                lifted = jnp.dot(x_s[c, r0:r0 + 2 * rows, :], w_s[slot], preferred_element_type=F32) + b_s[k]
                act_s[r0:r0 + 2 * rows, pl.ds(at, WIDE)] = gelu_tanh(lifted).astype(BF16)
            return inner

        lax.fori_loop(0, n_up, up_step, 0)

        @pl.when(c + 2 < chunks)
        def _():
            gather.forward(c + 2)

        @pl.when(c >= 2)
        def _():
            scatter.relay(c - 2)

        def down_step(k, inner):
            slot = landed(c, k)
            at = pl.multiple_of((k - n_up) * WIDE, WIDE)
            out_s[c, :, pl.ds(at, WIDE)] = jnp.dot(act_s[...], w_s[slot], preferred_element_type=F32).astype(BF16)
            return inner

        lax.fori_loop(n_up, n_tiles, down_step, 0)
        scatter.start(c)
        return carry

    lax.fori_loop(0, chunks, chunk, 0)
    scatter.close(mid_s, b_down[layer:layer + 1, :].astype(F32), h_out, h_sem, chunks, chunks - 2)
    for c in range(chunks):
        gather.drain(c)
    b_push.wait_send()


def run_mlp(layer, chunks, middle, norms, b_down, b_up, up, down, up_peer, down_peer):
    model = middle.shape[1]
    rows = middle.shape[0] // chunks
    ffn = up.shape[2]
    dims = (chunks, rows, model, ffn)
    flops = 2 * 4 * rows * chunks * model * ffn * 4
    return pl.pallas_call(
        functools.partial(mlp_kernel, layer, dims),
        out_shape=jax.ShapeDtypeStruct(middle.shape, BF16),
        in_specs=[ANY] + [VMEM] * 3 + [ANY] * 5,
        out_specs=ANY,
        scratch_shapes=[
            pltpu.VMEM((chunks, 4 * rows, model), BF16),
            pltpu.VMEM((chunks, 4 * rows, model), BF16),
            pltpu.VMEM((chunks, 3 * rows, model), BF16),
            pltpu.VMEM((4 * rows, 2 * ffn), BF16),
            pltpu.VMEM((WEIGHT_SLOTS, model, WIDE), BF16),
            pltpu.VMEM((chunks, rows, model), BF16),
            pltpu.VMEM((2 * ffn // WIDE, 1, WIDE), F32),
            pltpu.VMEM(b_up.shape, BF16),
            DMA((chunks, 4)),
            DMA((chunks, 4)),
            DMA((chunks, 6)),
            DMA((chunks, 6)),
            DMA((chunks,)),
            DMA((WEIGHT_SLOTS,)),
            DMA,
            DMA,
            DMA((chunks,)),
        ],
        compiler_params=pltpu.CompilerParams(vmem_limit_bytes=VMEM_LIMIT, collective_id=3 * layer + 2, has_side_effects=True),
        cost_estimate=pl.CostEstimate(flops=2 * flops, bytes_accessed=60_000_000, transcendentals=8 * rows * ffn),
        name=f"mlp_l{layer}",
    )(middle, norms, b_down, b_up, b_up, up, down, up_peer, down_peer)


def solution(mesh):
    row_spec = P('dp', 'tp', None)
    cache_spec = P(None, 'dp', None, 'tp', None)
    col_spec = P(None, None, 'tp')
    bias_spec = P(None, 'tp')
    in_specs = (row_spec, P('dp'), P('dp', None, None), P('dp', None, None), cache_spec, cache_spec, P('dp', None), P(), col_spec, bias_spec, col_spec, bias_spec, col_spec, bias_spec, P(None, 'tp', None), P(), col_spec, bias_spec, P(None, 'tp', None), P())
    out_specs = (row_spec, cache_spec, cache_spec, P('dp', None))

    def device_step(tokens, start_pos, cos_tab, sin_tab, key_cache, value_cache, slot_pos, norm_params, w_q, b_q, w_k, b_k, w_v, b_v, w_o, b_o, w_up, b_up, w_down, b_down):
        layers, _, window, _, hd = key_cache.shape
        cos, sin = cos_tab[0], sin_tab[0]
        kc = key_cache.reshape(layers, window, hd)
        vc = value_cache.reshape(layers, window, hd)
        hidden = tokens[0]
        fresh = []
        for layer in range(layers):
            q, kv_mine, kv_other, cache_mine, cache_peer, wo_peer, up_peer, down_peer, state = run_qkv(layer, CHUNKS, start_pos, hidden, norm_params, cos, sin, (w_q, w_k, w_v), (b_q, b_k, b_v), (kc, vc), w_o, w_up, w_down)
            middle, kv_rolled = run_attn(layer, start_pos, q, kv_mine, kv_other, cache_mine, cache_peer, state, w_o, wo_peer, hidden, b_o)
            hidden = run_mlp(layer, CHUNKS, middle, norm_params, b_down, b_up, w_up, w_down, up_peer, down_peer)
            fresh.append(kv_rolled)
        key_out = jnp.stack([f[0] for f in fresh]).reshape(key_cache.shape)
        value_out = jnp.stack([f[1] for f in fresh]).reshape(value_cache.shape)
        first_slot = start_pos[0] % window
        pos_out = (start_pos[0] + (jnp.arange(window, dtype=jnp.int32) - first_slot) % window)[None]
        return hidden[None], key_out, value_out, pos_out

    return jax.shard_map(device_step, mesh=mesh, in_specs=in_specs, out_specs=out_specs, check_vma=False)
```

time: 1120 us -> 1040 us (0.929)
  Pallas kernels: 1100 us -> 1030 us
    pallas_call x2, Pallas kernels: 339 us -> 271 us  [run_attn(): pl.pallas_call(functools.partial(attn_kernel, layer, dims), out_shape=(ja...]
where the time goes in v1:
time: 1040 us
  Pallas kernels  1030 us (99%)
    pallas_call x2, Pallas kernels, run_mlp(): pl.pallas_call(functools.partial(mlp_kernel, layer, dims), out_shape=jax....  493 us
    pallas_call x2, Pallas kernels, run_attn(): pl.pallas_call(functools.partial(attn_kernel, layer, dims), out_shape=(ja...  271 us
    pallas_call x2, Pallas kernels, run_qkv(): pl.pallas_call(functools.partial(qkv_kernel, layer, dims), out_shape=tupl...  265 us

profile of v1, /device:TPU:0, one launch (start us, length us, event | category | flops | bytes accessed | tf_op | source)
XLA Modules:
  0.0 1041.8 jit_solution(11980764398899347380)
XLA Ops:
  1.3 133.1 %qkv_l0.1 = (bf16[4,2,4,2,128,256]{5,4,3,2,1,0:T(8,128)(2,1)}, bf16[2,4096,256]{2,1,0:T(8,128)(2,1)}, bf16[2,4096,256]{2,1,0:T(8,128)(2,1)}, bf16[2,4096,256]{2,...) custom-call(s32[1]{0:T(128)} %copy.26.scal, ...), custom_call_target="tpu_custom_call" | custom-call | flops 120259084288 | bytes 20000000 | tf_op jit(solution)/shard_map/qkv_l0/pallas_call | solution.py:452
  134.3 134.9 %attn_l0.1 = (bf16[512,3584]{1,0:T(8,128)(2,1)}, bf16[2,4096,256]{2,1,0:T(8,128)(2,1)}) custom-call(s32[1]{0:T(128)} %copy.26.scal, bf16[4,2,4,2,128,256]{5,4,3,2,1,0:T(8,128)(2,1)} %get-tuple-element.26.refs_0_, bf16[2,4096,256]{2,1,0:T(8,128)(2,1)} %get-tuple-element.27.refs_1_, bf16[2,4096,256]{2,1,0:T(8,128)(2,1)} %get-tuple-element.28.refs_2_, ...), custom_call_target="tpu_custom_call" | custom-call | flops 49392123904 | bytes 30000000 | tf_op jit(solution)/shard_map/attn_l0/pallas_call | solution.py:672
  269.2 246.2 %mlp_l0.1.refs_0_.refs_8_ = bf16[512,3584]{1,0:T(8,128)(2,1)} custom-call(bf16[512,3584]{1,0:T(8,128)(2,1)} %get-tuple-element.33.refs_0_, bf16[2,4,3584]{2,1,0:T(4,128)(2,1)} %refs_1_.7, bf16[2,3584]{1,0:T(2,128)(2,1)} %refs_2_.3, bf16[2,1792]{1,0:T(2,128)(2,1)} %refs_4_.7, bf16[2,1792]{1,0:T(2,128)(2,1)} %refs_4_.7, bf16[2,3584,1792]{2,1,0:T(8,128)(2,1)} %refs_5_.7, ...), custom_call_target="tpu_custom_call" | custom-call | flops 210453397504 | bytes 60000000 | tf_op jit(solution)/shard_map/mlp_l0/pallas_call | solution.py:825
  515.4 131.4 %qkv_l1.1 = (bf16[4,2,4,2,128,256]{5,4,3,2,1,0:T(8,128)(2,1)}, bf16[2,4096,256]{2,1,0:T(8,128)(2,1)}, bf16[2,4096,256]{2,1,0:T(8,128)(2,1)}, bf16[2,4096,256]{2,...) custom-call(s32[1]{0:T(128)} %copy.26.scal, ...), custom_call_target="tpu_custom_call" | custom-call | flops 120259084288 | bytes 20000000 | tf_op jit(solution)/shard_map/qkv_l1/pallas_call | solution.py:452
  646.9 136.3 %attn_l1.1 = (bf16[512,3584]{1,0:T(8,128)(2,1)}, bf16[2,4096,256]{2,1,0:T(8,128)(2,1)}) custom-call(s32[1]{0:T(128)} %copy.26.scal, bf16[4,2,4,2,128,256]{5,4,3,2,1,0:T(8,128)(2,1)} %get-tuple-element.36.refs_0_, bf16[2,4096,256]{2,1,0:T(8,128)(2,1)} %get-tuple-element.37.refs_1_, bf16[2,4096,256]{2,1,0:T(8,128)(2,1)} %get-tuple-element.38.refs_2_, ...), custom_call_target="tpu_custom_call" | custom-call | flops 49392123904 | bytes 30000000 | tf_op jit(solution)/shard_map/attn_l1/pallas_call | solution.py:672
  783.2 0.0 copy-start
  783.2 2.6 fusion.3
  785.9 0.8 copy-done
  786.7 0.3 fusion.2
  787.0 3.7 maximum_bitcast_fusion
  790.7 246.3 %mlp_l1.1 = bf16[512,3584]{1,0:T(8,128)(2,1)} custom-call(bf16[512,3584]{1,0:T(8,128)(2,1)} %get-tuple-element.43.refs_0_, bf16[2,4,3584]{2,1,0:T(4,128)(2,1)} %refs_1_.7, bf16[2,3584]{1,0:T(2,128)(2,1)} %refs_2_.3, bf16[2,1792]{1,0:T(2,128)(2,1)} %refs_4_.7, bf16[2,1792]{1,0:T(2,128)(2,1)} %refs_4_.7, bf16[2,3584,1792]{2,1,0:T(8,128)(2,1)} %refs_5_.7, ...), custom_call_target="tpu_custom_call" | custom-call | flops 210453397504 | bytes 60000000 | tf_op jit(solution)/shard_map/mlp_l1/pallas_call | solution.py:825
  1037.0 0.7 fusion
  1037.7 4.1 copy.27
Async XLA Ops:
  783.2 3.5 copy-start

commit v2 on v1

v2 whole, which is shorter than its diff:
```python
import functools

import jax
import jax.numpy as jnp
from jax import lax
from jax.experimental import pallas as pl
from jax.experimental.pallas import tpu as pltpu
from jax.sharding import PartitionSpec as P

NORM_EPS = 1e-5
LOG2E = 1.4426950408889634
CHUNKS = 4
KEY_TILE = 512
LANES = 128
WIDE = 512
ROW_BLOCK = 16
PAIR = 2
GROUP = 4
WEIGHT_SLOTS = 3
ROLL_ROWS = 256
ROLL_SLOTS = 4
EARLY = 2
LOWEST = -3.3e38
VMEM_LIMIT = 67_043_328
BF16 = jnp.bfloat16
F32 = jnp.float32
MESH = pl.DeviceIdType.MESH

ANY = pl.BlockSpec(memory_space=pl.ANY)
SMEM = pl.BlockSpec(memory_space=pltpu.SMEM)
VMEM = pl.BlockSpec(memory_space=pltpu.VMEM)
DMA = pltpu.SemaphoreType.DMA


def vm(*shape, dtype=BF16):
    return pltpu.VMEM(shape, dtype)


def dma(*shape):
    return DMA(shape) if shape else DMA


def whole(ref, sem):
    pltpu.make_async_copy(ref, ref, sem).wait()


def one_row(ref, n):
    return ref[pl.ds(n, 1), :].astype(F32)


def gelu_tanh(x):
    inner = 0.7978845608028654 * (x + 0.044715 * (x * x * x))
    return 0.5 * x * (1.0 + jnp.tanh(inner))


def normalized(values, gain, shift):
    centered = values - jnp.mean(values, axis=-1, keepdims=True)
    variance = jnp.mean(centered * centered, axis=-1, keepdims=True)
    return (centered * lax.rsqrt(variance + NORM_EPS) * gain + shift).astype(BF16)


def rotate(planes, put, window, shift, first, last):
    def tile(n, carry):
        want = lax.broadcasted_iota(jnp.int32, (ROLL_ROWS, 1), 0) + (n * ROLL_ROWS + shift)
        want = jnp.where(want >= window, want - window, want)
        pick = jnp.where(lax.broadcasted_iota(jnp.int32, (1, window), 1) == want, 1.0, 0.0).astype(BF16)
        put(n, [jnp.dot(pick, planes(k), preferred_element_type=F32).astype(BF16) for k in range(PAIR)])
        return carry

    lax.fori_loop(first, last, tile, 0)


def reset_state(st_s, w):
    for g in range(PAIR):
        st_s[w, g, :, 0:LANES] = jnp.full((st_s.shape[2], LANES), LOWEST, F32)
        st_s[w, g, :, LANES:] = jnp.zeros((st_s.shape[2], st_s.shape[3] - LANES), F32)


def flash_step(st_s, w, s_s, scale, mask, values, next_scores):
    for g in range(PAIR):
        s = jnp.where(mask, s_s[g] * scale, -jnp.inf)
        s_next = next_scores(g)
        m_prev = st_s[w, g, :, 0:LANES]
        m_next = jnp.maximum(m_prev, jnp.max(s, axis=1, keepdims=True))
        e = jnp.exp2(s - jnp.concatenate([m_next] * (s.shape[1] // LANES), axis=1))
        alpha = jnp.exp2(m_prev - m_next)
        total = st_s[w, g, :, LANES:2 * LANES] * alpha
        for k in range(s.shape[1] // LANES):
            total = total + e[:, k * LANES:(k + 1) * LANES]
        st_s[w, g, :, LANES:2 * LANES] = total
        st_s[w, g, :, 0:LANES] = m_next
        mixed = jnp.dot(e.astype(BF16), values(g), preferred_element_type=F32)
        st_s[w, g, :, 2 * LANES:] = st_s[w, g, :, 2 * LANES:] * jnp.concatenate([alpha] * (mixed.shape[1] // LANES), axis=1) + mixed
        s_s[g] = s_next


def score_tile(queries, keys):
    return lax.dot_general(queries, keys, (((1,), (1,)), ((), ())), preferred_element_type=F32)


class Place:
    def __init__(self):
        me = lax.axis_index('tp')
        self.core = lax.rem(me, 2)
        self.xb = lax.rem(lax.div(me, 2), 2)
        self.yb = lax.div(me, 4)
        self.peer = me + 1 - 2 * self.core
        self.x = me + 2 - 4 * self.xb
        self.y = me + 4 - 8 * self.yb

    def member(self, i):
        xb = self.xb + lax.rem(i, 2) * (1 - 2 * self.xb)
        yb = self.yb + lax.div(i, 2) * (1 - 2 * self.yb)
        return yb * 2 + xb

    def barrier(self, others):
        sem = pltpu.get_barrier_semaphore()
        for other in others:
            pl.semaphore_signal(sem, inc=1, device_id={'tp': other}, device_id_type=MESH)
        pl.semaphore_wait(sem, len(others))


def remote(src, dst, send_sem, recv_sem, other):
    return pltpu.make_async_remote_copy(src_ref=src, dst_ref=dst, send_sem=send_sem, recv_sem=recv_sem, device_id={'tp': other}, device_id_type=MESH)


class Gather:
    def __init__(self, place, x_s, send, recv, rows):
        self.place, self.x_s, self.send, self.recv, self.rows = place, x_s, send, recv, rows

    def copy(self, c, kind):
        r, h = self.rows, self.rows // 2
        src, dst, size, other = ((0, r, r, self.place.x), (0, 2 * r, r, self.place.y), (r, 3 * r, h, self.place.y), (2 * r + h, 3 * r + h, h, self.place.x))[kind]
        return remote(self.x_s.at[c, pl.ds(src, size)], self.x_s.at[c, pl.ds(dst, size)], self.send.at[c, kind], self.recv.at[c, kind], other)

    def start(self, c):
        self.copy(c, 0).start()
        self.copy(c, 1).start()

    def forward(self, c):
        self.copy(c, 0).wait_recv()
        self.copy(c, 2).start()
        self.copy(c, 1).wait_recv()
        self.copy(c, 3).start()

    def finish(self, c):
        self.copy(c, 2).wait_recv()
        self.copy(c, 3).wait_recv()

    def drain(self, c):
        for kind in range(4):
            self.copy(c, kind).wait_send()


class Scatter:
    def __init__(self, place, out_s, land_s, send, recv, rows, shift):
        self.place, self.out_s, self.land_s, self.send, self.recv, self.rows, self.shift = place, out_s, land_s, send, recv, rows, shift

    def copy(self, c, kind):
        r, h = self.rows, self.rows // 2
        x, y = self.place.x, self.place.y
        src, dst, other = ((3 * r, 2 * r, x), (3 * r + h, 2 * r + h, y), (r, 0, x), (2 * r + h, r + h, y), (r + h, h, x), (2 * r, r, y))[kind]
        return remote(self.out_s.at[c + self.shift, pl.ds(src, h)], self.land_s.at[c, pl.ds(dst, h)], self.send.at[c, kind], self.recv.at[c, kind], other)

    def start(self, c):
        for kind in range(4):
            self.copy(c, kind).start()

    def add(self, c, kind, src, dst):
        self.copy(c, kind).wait_recv()
        slot = c + self.shift

        def block(n, carry):
            at = pl.multiple_of(n * ROW_BLOCK, ROW_BLOCK)
            mine = self.out_s[slot, pl.ds(dst + at, ROW_BLOCK), :].astype(F32)
            came = self.land_s[c, pl.ds(src + at, ROW_BLOCK), :].astype(F32)
            self.out_s[slot, pl.ds(dst + at, ROW_BLOCK), :] = (mine + came).astype(BF16)
            return carry

        lax.fori_loop(0, self.rows // 2 // ROW_BLOCK, block, 0)

    def relay(self, c, settled=None):
        r, h = self.rows, self.rows // 2
        self.add(c, 0, 2 * r, 2 * r)
        self.add(c, 1, 2 * r + h, r + h)
        if settled is not None:
            @pl.when(settled >= 0)
            def _():
                self.drain(settled)

        self.copy(c, 5).start()
        self.copy(c, 4).start()

    def finish(self, c):
        for kind in range(2, 6):
            self.copy(c, kind).wait_recv()

    def drain(self, c):
        for kind in range(6):
            self.copy(c, kind).wait_send()

    def total(self, c, at):
        own = self.out_s[c + self.shift, pl.ds(at, ROW_BLOCK), :].astype(F32)
        came = [self.land_s[c, pl.ds(k * self.rows + at, ROW_BLOCK), :].astype(F32) for k in range(PAIR)]
        return own + came[0] + came[1]


def qkv_kernel(layer, dims, scal, *refs):
    chunks, rows, model, hd, window = dims
    (hidden, norms, cos, sin, wq, wk, wv, bq, bk, bv, bq_push, bk_push, bv_push, kc, vc, wo, w_up, w_down,
     q_out, kv_mine, kv_other, cache_mine, cache_peer, wo_peer, up_peer, down_peer, state,
     x_s, h_s, t_s, w_s, b_s, bq_s, bk_s, bv_s, oq_s, okv_s, old_s, oldp_s, st_s, s_s,
     ag_send, ag_recv, h_sem, t_sem, w_sem, wr_send, wr_recv, p_send, p_recv, q_sem, kv_sem, kr_send, kr_recv, raw_sem, old_sem, st_sem) = refs
    place = Place()
    block = rows * chunks
    tall = PAIR * rows
    tile = KEY_TILE
    tiles = window // tile
    scale = LOG2E * hd ** -0.5
    floor = window - 1 - scal[0]
    loads = [pltpu.make_async_copy(hidden.at[pl.ds(c * rows, rows)], h_s.at[c], h_sem.at[c]) for c in range(chunks)]
    for copy in loads:
        copy.start()
    for k, cache in enumerate((kc, vc)):
        pltpu.make_async_copy(cache.at[layer], okv_s.at[pl.ds(k * window, window)], raw_sem).start()
    place.barrier((place.x, place.y, place.peer))
    gather = Gather(place, x_s, ag_send, ag_recv, rows)
    parts = ((wq.at[layer], 0, 0, 2 * hd), (wk.at[layer], 1, 0, hd), (wv.at[layer], 1, hd, hd))
    w_local = [pltpu.make_async_copy(src, w_s.at[t, :, pl.ds(at, n)], w_sem.at[k]) for k, (src, t, at, n) in enumerate(parts)]
    w_remote = [remote(src, w_s.at[2 + t, :, pl.ds(at, n)], wr_send.at[k], wr_recv.at[k], place.peer) for k, (src, t, at, n) in enumerate(parts)]
    b_remote = [remote(src, dst, wr_send.at[3 + k], wr_recv.at[3 + k], place.peer) for k, (src, dst) in enumerate(zip((bq_push, bk_push, bv_push), (bq_s, bk_s, bv_s)))]
    landing = (wo_peer, up_peer, down_peer)
    pushes = [remote(src.at[layer], dst, p_send.at[k], p_recv.at[k], place.peer) for k, (src, dst) in enumerate(zip((wo, w_up, w_down), landing))]
    old_push = remote(old_s, oldp_s, p_send.at[3], p_recv.at[3], place.peer)
    old_store = [pltpu.make_async_copy(src, dst, old_sem.at[k]) for k, (src, dst) in enumerate(((old_s, cache_mine), (oldp_s, cache_peer)))]
    gain = one_row(norms.at[layer], 0)
    shift = one_row(norms.at[layer], 1)

    def send_own(c):
        loads[c].wait()

        def norm_block(n, carry):
            at = pl.multiple_of(n * ROW_BLOCK, ROW_BLOCK)
            x_s[c, pl.ds(at, ROW_BLOCK), :] = normalized(h_s[c, pl.ds(at, ROW_BLOCK), :].astype(F32), gain, shift)
            return carry

        lax.fori_loop(0, rows // ROW_BLOCK, norm_block, 0)
        gather.start(c)

    def chunk_pos(c, i):
        return pl.multiple_of((place.member(i) * 2 + place.core) * block + c * rows, rows)

    def kv_row(c, kv, g):
        return pl.multiple_of(((c * PAIR + kv) * PAIR + g) * GROUP * rows, rows)

    def q_row(c, g, i):
        return pl.multiple_of(((c * PAIR + g) * GROUP + i) * tall, rows)

    send_own(0)
    send_own(1)
    for copy in b_remote + w_remote + w_local + pushes:
        copy.start()
    for c in range(chunks):
        for i in range(GROUP):
            for k, tab in enumerate((cos, sin)):
                pltpu.make_async_copy(tab.at[pl.ds(chunk_pos(c, i), rows)], t_s.at[c, k, pl.ds(i * rows, rows)], t_sem.at[c]).start()
    whole(okv_s, raw_sem)
    first_slot = lax.rem(scal[0], window)
    roll_tiles = window // ROLL_ROWS

    def raw_plane(k):
        return okv_s[k * window:(k + 1) * window, :]

    def put_old(n, turned):
        for k in range(PAIR):
            old_s[pl.ds(pl.multiple_of(k * window + n * ROLL_ROWS, ROLL_ROWS), ROLL_ROWS), :] = turned[k]

    rotate(raw_plane, put_old, window, first_slot, 0, roll_tiles // 3)
    gather.forward(0)
    send_own(2)
    rotate(raw_plane, put_old, window, first_slot, roll_tiles // 3, roll_tiles)
    old_push.start()
    old_store[0].start()
    gather.forward(1)
    for copy in b_remote:
        copy.wait_recv()
    for g, (for_q, for_k, for_v) in enumerate(((bq, bk, bv), (bq_s, bk_s, bv_s))):
        b_s[PAIR * g] = one_row(for_q, layer)
        b_s[PAIR * g + 1, :, :hd] = one_row(for_k, layer)
        b_s[PAIR * g + 1, :, hd:] = one_row(for_v, layer)

    def project(c, i0, count):
        r0, n = i0 * rows, count * rows

        def rope(u):
            turned = jnp.concatenate([-u[:, hd // 2:], u[:, :hd // 2]], axis=1)
            return (u * t_s[c, 0, r0:r0 + n, :] + turned * t_s[c, 1, r0:r0 + n, :]).astype(BF16)

        def side(g, carry):
            u = jnp.dot(x_s[c, r0:r0 + n, :], w_s[PAIR * g], preferred_element_type=F32) + b_s[PAIR * g]
            for h in range(PAIR):
                turned = rope(u[:, h * hd:(h + 1) * hd])
                for i in range(count):
                    oq_s[pl.ds(pl.multiple_of(q_row(c, g, i0 + i) + h * rows, rows), rows), :] = turned[i * rows:(i + 1) * rows]
            u = jnp.dot(x_s[c, r0:r0 + n, :], w_s[PAIR * g + 1], preferred_element_type=F32) + b_s[PAIR * g + 1]
            okv_s[pl.ds(pl.multiple_of(kv_row(c, 0, g) + r0, rows), n), :] = rope(u[:, :hd])
            okv_s[pl.ds(pl.multiple_of(kv_row(c, 1, g) + r0, rows), n), :] = u[:, hd:].astype(BF16)
            return carry

        lax.fori_loop(0, 2, side, 0)

    def q_copy(c):
        part = pl.ds(q_row(c, 0, 0), PAIR * GROUP * tall)
        return pltpu.make_async_copy(oq_s.at[part], q_out.at[part], q_sem.at[c])

    def kv_copies(c):
        planes = (kv_mine, kv_other)
        made = []
        for kv in range(PAIR):
            for g in range(PAIR):
                for i in range(GROUP):
                    src = okv_s.at[pl.ds(pl.multiple_of(kv_row(c, kv, g) + i * rows, rows), rows)]
                    at = pl.ds(pl.multiple_of(kv * window + chunk_pos(c, i), rows), rows)
                    made.append(pltpu.make_async_copy(src, planes[g].at[at], kv_sem.at[c]))
                    made.append(remote(src, planes[1 - g].at[at], kr_send.at[c], kr_recv.at[c], place.peer))
        return made

    def old_tile(g, kv, at):
        return (old_s, oldp_s)[g][pl.ds(pl.multiple_of(kv * window + at, tile), tile), :]

    def queries(c, i, g):
        return oq_s[pl.ds(q_row(c, g, i), tall), :]

    def state_copy(b):
        return pltpu.make_async_copy(st_s.at[lax.rem(b, PAIR)], state.at[b], st_sem.at[lax.rem(b, PAIR)])

    def start_old(c, i):
        at = pl.multiple_of(lax.div(chunk_pos(c, i), tile) * tile, tile)
        for g in range(PAIR):
            s_s[g] = score_tile(queries(c, i, g), old_tile(g, 0, at))

    def attend_old(c, i):
        b = c * GROUP + i
        w = lax.rem(b, PAIR)
        j0 = chunk_pos(c, i)
        diag = lax.div(j0, tile)
        i_next = jnp.minimum(i + 1, 3)
        diag_next = lax.div(chunk_pos(c, i_next), tile)

        @pl.when(b >= 2)
        def _():
            state_copy(b - 2).wait()

        reset_state(st_s, w)

        def step(t, by_row):
            at = pl.multiple_of(t * tile, tile)
            last = t + 1 == tiles
            n_at = pl.multiple_of(jnp.where(last, diag_next, t + 1) * tile, tile)
            n_i = jnp.where(last, i_next, i)
            age = lax.broadcasted_iota(jnp.int32, (1, tile), 1) + at
            if by_row:
                row = lax.rem(lax.broadcasted_iota(jnp.int32, (tall, 1), 0), rows) + j0
                mask = age > jnp.maximum(row, floor)
            else:
                mask = age > floor
            flash_step(st_s, w, s_s, scale, mask, lambda g: old_tile(g, 1, at), lambda g: score_tile(queries(c, n_i, g), old_tile(g, 0, n_at)))

        step(diag, True)

        def younger(t, carry):
            @pl.when(t > diag)
            def _():
                step(t, False)

            return carry

        lax.fori_loop(1, tiles, younger, 0)
        state_copy(b).start()

    def chunk(c, carry):
        whole(t_s.at[c], t_sem.at[c])

        @pl.when(c == 0)
        def _():
            for copy in w_local:
                copy.wait()
            for copy in w_remote:
                copy.wait_recv()

        project(c, 0, 3)
        gather.finish(c)
        project(c, 3, 1)
        q_copy(c).start()
        for copy in kv_copies(c):
            copy.start()

        @pl.when(c == 0)
        def _():
            old_push.wait_recv()
            old_store[1].start()

        @pl.when(lax.rem(c, 2) == 0)
        def _():
            early = lax.div(c, 2)
            start_old(early, 0)

            def one(i, inner):
                @pl.when(jnp.logical_and(c == 2, i == 3))
                def _():
                    gather.forward(3)

                attend_old(early, i)
                return inner

            lax.fori_loop(0, 4, one, 0)

        @pl.when(c == 0)
        def _():
            gather.forward(2)
            send_own(3)

        return carry

    lax.fori_loop(0, chunks, chunk, 0)
    for copy in w_remote + b_remote:
        copy.wait_send()

    def settle(c, carry):
        q_copy(c).wait()
        part = okv_s.at[pl.ds(kv_row(c, 0, 0), PAIR * PAIR * GROUP * rows)]
        whole(part, kv_sem.at[c])
        remote(part, part, kr_send.at[c], kr_recv.at[c], place.peer).wait_send()
        remote(part, part, kr_send.at[c], kr_recv.at[c], place.peer).wait_recv()
        gather.drain(c)
        return carry

    lax.fori_loop(0, chunks, settle, 0)
    for copy in pushes:
        copy.wait_send()
        copy.wait_recv()
    old_push.wait_send()
    for copy in old_store:
        copy.wait()
    for b in (GROUP * EARLY - 2, GROUP * EARLY - 1):
        state_copy(b).wait()


def run_qkv(layer, chunks, scal, hidden, norms, cos, sin, weights, biases, caches, w_o, w_up, w_down):
    model = hidden.shape[1]
    rows = hidden.shape[0] // chunks
    hd = cos.shape[1]
    window = cos.shape[0]
    dims = (chunks, rows, model, hd, window)
    flops = 2 * 4 * rows * chunks * model * 8 * hd
    planes = (PAIR * window, hd)
    shapes = [(chunks * PAIR * GROUP * PAIR * rows, hd)] + [planes] * 4 + [w.shape[1:] for w in (w_o, w_up, w_down)]
    state = (GROUP * EARLY, PAIR, PAIR * rows, PAIR * LANES + hd)
    return pl.pallas_call(
        functools.partial(qkv_kernel, layer, dims),
        out_shape=tuple(jax.ShapeDtypeStruct(s, BF16) for s in shapes) + (jax.ShapeDtypeStruct(state, F32),),
        in_specs=[SMEM, ANY, VMEM] + [ANY] * 5 + [VMEM] * 3 + [ANY] * 8,
        out_specs=(ANY,) * (len(shapes) + 1),
        scratch_shapes=[
            vm(chunks, GROUP * rows, model),
            vm(chunks, rows, model),
            vm(chunks, PAIR, GROUP * rows, hd, dtype=F32),
            vm(GROUP, model, PAIR * hd),
            vm(GROUP, 1, PAIR * hd, dtype=F32),
            *(vm(*b.shape) for b in biases),
            vm(*shapes[0]),
            vm(chunks * PAIR * PAIR * GROUP * rows, hd),
            vm(*planes),
            vm(*planes),
            vm(PAIR, *state[1:], dtype=F32),
            vm(PAIR, PAIR * rows, KEY_TILE, dtype=F32),
            dma(chunks, GROUP),
            dma(chunks, GROUP),
            dma(chunks),
            dma(chunks),
            dma(3),
            dma(6),
            dma(6),
            dma(GROUP),
            dma(GROUP),
            dma(chunks),
            dma(chunks),
            dma(chunks),
            dma(chunks),
            dma(),
            dma(PAIR),
            dma(PAIR),
        ],
        compiler_params=pltpu.CompilerParams(vmem_limit_bytes=VMEM_LIMIT, collective_id=PAIR * layer, has_side_effects=True),
        cost_estimate=pl.CostEstimate(flops=4 * flops, bytes_accessed=20_000_000, transcendentals=0),
        name=f"qkv_l{layer}",
    )(scal, hidden, norms, cos, sin, *weights, *biases, *biases, *caches, w_o, w_up, w_down)


def block_kernel(layer, dims, scal, *refs):
    chunks, rows, model, hd, window, ffn = dims
    (q, kv_mine, kv_other, cache_mine, cache_peer, state, wo, wo_peer, hidden, norms, b_o, b_down, b_up, b_push, up, down, up_peer, down_peer,
     h_out, kv_rolled,
     big_s, q_s, s_s, mix_s, wo_s, xo_s, land_s, mid_s, st_s, b_s, bp_s,
     r1_send, r1_recv, r2_send, r2_recv, ag_send, ag_recv, new_sem, old_sem, q_sem, wo_sem, h_sem, st_sem, w_sem, b_send, b_recv, o_sem, f_sem) = refs
    place = Place()
    start_pos = scal[0]
    block = rows * chunks
    tall = PAIR * rows
    tile = KEY_TILE
    tiles = window // tile
    scale = LOG2E * hd ** -0.5

    def region(g, new):
        return jnp.where(new, (3 - g) * window, g * window)

    def load_planes(src, base, sem):
        for k in range(PAIR):
            pltpu.make_async_copy(src.at[pl.ds(k * window, window)], big_s.at[pl.ds(base, window), pl.ds(k * hd, hd)], sem).start()

    q_rows = PAIR * GROUP * tall

    def q_copy(c):
        slot = lax.rem(c, PAIR)
        src, dst = (pl.ds(pl.multiple_of(n * q_rows, rows), q_rows) for n in (c, slot))
        return pltpu.make_async_copy(q.at[src], q_s.at[dst], q_sem.at[slot])

    q_copy(jnp.int32(0)).start()
    q_copy(jnp.int32(1)).start()
    load_planes(kv_mine, 3 * window, new_sem)
    load_planes(kv_other, PAIR * window, new_sem)

    def pick(k):
        return jnp.where(k == 0, 3, jnp.where(k == 3, 0, k))

    def state_copy(b):
        slot = lax.rem(b, PAIR)
        return pltpu.make_async_copy(state.at[lax.div(b, GROUP) * GROUP + pick(lax.rem(b, GROUP))], st_s.at[slot], st_sem.at[slot])

    for b in range(PAIR):
        state_copy(jnp.int32(b)).start()
    pltpu.make_async_copy(wo.at[layer], wo_s.at[pl.ds(0, PAIR * hd)], wo_sem).start()
    pltpu.make_async_copy(wo_peer, wo_s.at[pl.ds(PAIR * hd, PAIR * hd)], wo_sem).start()
    load_planes(cache_mine, 0, old_sem)
    load_planes(cache_peer, window, old_sem)
    for c in range(chunks):
        pltpu.make_async_copy(hidden.at[pl.ds(c * rows, rows)], mid_s.at[c], h_sem).start()
    place.barrier((place.x, place.y, place.peer))
    b_copy = remote(b_push, bp_s, b_send, b_recv, place.peer)
    b_copy.start()
    first = Scatter(place, xo_s, land_s, r1_send, r1_recv, rows, 1)
    second = Scatter(place, xo_s, land_s, r2_send, r2_recv, rows, 0)
    gather = Gather(place, xo_s, ag_send, ag_recv, rows)
    first_slot = lax.rem(start_pos, window)
    floor = window - 1 - start_pos

    def first_row(c, i):
        return (place.member(i) * PAIR + place.core) * block + c * rows

    def tile_at(diag, n):
        is_new = jnp.logical_or(n == 0, jnp.logical_and(n >= 2, n - 2 < diag))
        t = jnp.where(n < 2, diag, jnp.where(is_new, n - 2, n - 1))
        return is_new, t * tile

    def tile_of(g, is_new, at, kv):
        return big_s[pl.ds(pl.multiple_of(region(g, is_new) + at, tile), tile), kv * hd:(kv + 1) * hd]

    def scores(c, i, g, is_new, at):
        r0 = pl.multiple_of(((lax.rem(c, PAIR) * PAIR + g) * GROUP + i) * tall, rows)
        return score_tile(q_s[pl.ds(r0, tall), :], tile_of(g, is_new, at, 0))

    q_copy(jnp.int32(0)).wait()
    whole(big_s.at[pl.ds(0, PAIR * window)], new_sem)
    for g in range(PAIR):
        s_s[g] = scores(jnp.int32(0), 3, g, True, lax.div(first_row(0, 3), tile) * tile)

    def attend(c, k):
        i = pick(k)
        b = c * GROUP + k
        w = lax.rem(b, PAIR)
        late = c >= EARLY
        j0 = first_row(c, i)
        diag = lax.div(j0, tile)
        count = jnp.where(late, tiles + 1, diag + 2)
        end = k == 3
        c_next = jnp.minimum(jnp.where(end, c + 1, c), chunks - 1)
        i_next = pick(jnp.where(end, 0, k + 1))
        next_at = lax.div(first_row(c_next, i_next), tile) * tile

        @pl.when(late)
        def _():
            reset_state(st_s, w)

        @pl.when(jnp.logical_not(late))
        def _():
            state_copy(b).wait()

        def step(n):
            is_new, at = tile_at(diag, n)
            following = jnp.where(jnp.logical_and(n == 0, jnp.logical_not(late)), 2, n + 1)
            last = following == count
            new_next, at_next = tile_at(diag, following)
            new_next = jnp.logical_or(last, new_next)
            at_next = jnp.where(last, next_at, at_next)
            nc = jnp.where(last, c_next, c)
            ni = jnp.where(last, i_next, i)
            col = lax.broadcasted_iota(jnp.int32, (1, tile), 1) + at
            row = lax.rem(lax.broadcasted_iota(jnp.int32, (tall, 1), 0), rows) + j0
            if not isinstance(n, int):
                mask = col > jnp.where(is_new, -1, floor)
            elif n == 0:
                mask = col <= row
            else:
                mask = col > jnp.maximum(row, floor)
            flash_step(st_s, w, s_s, scale, mask, lambda g: tile_of(g, is_new, at, 1), lambda g: scores(nc, ni, g, new_next, at_next))

        step(0)

        @pl.when(late)
        def _():
            step(1)

        def further(n, carry):
            @pl.when(n < count)
            def _():
                step(n)

            return carry

        lax.fori_loop(2, tiles + 1, further, 0)
        for g in range(PAIR):
            total = jnp.sum(st_s[w, g, :, LANES:PAIR * LANES], axis=1, keepdims=True)
            out = (st_s[w, g, :, PAIR * LANES:] / total).astype(BF16)
            for h in range(PAIR):
                n = PAIR * g + h
                mix_s[:, n * hd:(n + 1) * hd] = out[h * rows:(h + 1) * rows]

        @pl.when(b + PAIR < GROUP * EARLY)
        def _():
            state_copy(b + PAIR).start()

        @pl.when(b == 0)
        def _():
            whole(wo_s, wo_sem)

        r0 = pl.multiple_of(i * rows, rows)
        for n in range(model // WIDE):
            cols = slice(n * WIDE, (n + 1) * WIDE)
            xo_s[c + 1, pl.ds(r0, rows), cols] = jnp.dot(mix_s[...], wo_s[:, cols], preferred_element_type=F32).astype(BF16)

        @pl.when(k == 0)
        def _():
            first.copy(c, 0).start()
            first.copy(c, 1).start()

        for kind in (2, 3):
            @pl.when(k == kind - 1)
            def _():
                first.copy(c, kind).start()

    gain = one_row(norms.at[layer], 2)
    shift = one_row(norms.at[layer], 3)
    bias_o = one_row(b_o, layer)
    bias_d = one_row(b_down, layer)

    def open_mlp(c):
        first.finish(c)

        def rows_at(n, carry):
            at = pl.multiple_of(n * ROW_BLOCK, ROW_BLOCK)
            middle = (mid_s[c, pl.ds(at, ROW_BLOCK), :].astype(F32) + first.total(c, at) + bias_o).astype(BF16)
            mid_s[c, pl.ds(at, ROW_BLOCK), :] = middle
            xo_s[c, pl.ds(at, ROW_BLOCK), :] = normalized(middle.astype(F32), gain, shift)
            return carry

        lax.fori_loop(0, rows // ROW_BLOCK, rows_at, 0)
        gather.start(c)

    def attend_chunk(c, carry):
        @pl.when(c == EARLY)
        def _():
            whole(big_s.at[pl.ds(0, PAIR * window)], old_sem)
            whole(mid_s, h_sem)

        def one(k, inner):
            @pl.when(jnp.logical_and(k == 3, c + 1 < chunks))
            def _():
                q_copy(c + 1).wait()

            attend(c, k)

            @pl.when(jnp.logical_and(k == 1, c >= 1))
            def _():
                first.relay(c - 1, c - 2)

            return inner

        lax.fori_loop(0, GROUP, one, 0)

        @pl.when(c + PAIR < chunks)
        def _():
            q_copy(c + PAIR).start()

        @pl.when(c >= 2)
        def _():
            open_mlp(c - 2)

        return carry

    lax.fori_loop(0, chunks, attend_chunk, 0)

    n_up = PAIR * ffn // WIDE
    n_tiles = n_up + model // WIDE
    sub = WIDE // PAIR
    n_sub = ffn // sub
    act = wo_s.at[pl.ds(0, GROUP * rows)]
    ups = (up.at[layer], up_peer)
    downs = (down.at[layer], down_peer)

    def slot_at(c, k):
        slot = lax.rem(c * n_tiles + k, WEIGHT_SLOTS)
        return slot, pl.multiple_of(slot * model, WIDE)

    def fetch(c, k):
        over = k >= n_tiles
        k = jnp.where(over, k - n_tiles, k)
        c = jnp.where(over, c + 1, c)
        slot, base = slot_at(c, k)

        @pl.when(c < chunks)
        def _():
            for part in range(PAIR):
                n = PAIR * k + part
                for side in range(PAIR):
                    @pl.when(jnp.logical_and(n >= side * n_sub, n < (side + 1) * n_sub))
                    def _():
                        at = pl.multiple_of((n - side * n_sub) * sub, sub)
                        pltpu.make_async_copy(ups[side].at[:, pl.ds(at, sub)], big_s.at[pl.ds(base, model), pl.ds(part * sub, sub)], w_sem.at[slot]).start()

            @pl.when(k >= n_up)
            def _():
                at = pl.multiple_of((k - n_up) * WIDE, WIDE)
                for side in range(PAIR):
                    dst = big_s.at[pl.ds(pl.multiple_of(base + side * ffn, sub), ffn)]
                    pltpu.make_async_copy(downs[side].at[:, pl.ds(at, WIDE)], dst, w_sem.at[slot]).start()

    def landed(c, k):
        slot, base = slot_at(c, k)
        whole(big_s.at[pl.ds(base, model)], w_sem.at[slot])
        fetch(c, k + WEIGHT_SLOTS - 1)
        return big_s[pl.ds(base, model), :]

    for k in range(WEIGHT_SLOTS - 1):
        fetch(jnp.int32(0), jnp.int32(k))
    roll_tiles = window // ROLL_ROWS

    def new_plane(k):
        return big_s[3 * window:, k * hd:(k + 1) * hd]

    stage = WEIGHT_SLOTS * model

    def stage_at(n):
        slot = lax.rem(n, ROLL_SLOTS)
        return slot, pl.ds(pl.multiple_of(stage + slot * ROLL_ROWS, ROLL_ROWS), ROLL_ROWS)

    def staged(n):
        slot, at = stage_at(n)
        whole(big_s.at[at], f_sem.at[slot])

    def put_new(n, turned):
        slot, at = stage_at(n)

        @pl.when(n >= ROLL_SLOTS)
        def _():
            staged(n)

        for k in range(PAIR):
            cols = slice(k * hd, (k + 1) * hd)
            big_s[at, cols] = turned[k]
            dst = pl.ds(pl.multiple_of(k * window + n * ROLL_ROWS, ROLL_ROWS), ROLL_ROWS)
            pltpu.make_async_copy(big_s.at[at, cols], kv_rolled.at[dst], f_sem.at[slot]).start()

    rotate(new_plane, put_new, window, window - first_slot, 0, roll_tiles // PAIR)
    gather.forward(0)
    rotate(new_plane, put_new, window, window - first_slot, roll_tiles // PAIR, roll_tiles)
    first.relay(chunks - 1, chunks - 2)
    b_copy.wait_recv()
    for n in range(PAIR * n_sub):
        src = b_up if n < n_sub else bp_s
        at = n % n_sub * sub
        b_s[n // PAIR, :, n % PAIR * sub:(n % PAIR + 1) * sub] = one_row(src, layer)[:, at:at + sub]
    open_mlp(2)
    gather.forward(1)
    open_mlp(3)

    def mlp_chunk(c, carry):
        gather.finish(c)

        def up_step(k, inner):
            weights = landed(c, k)
            for top in range(PAIR):
                r0 = top * tall
                lifted = jnp.dot(xo_s[c, r0:r0 + tall, :], weights, preferred_element_type=F32) + b_s[k]
                act[r0:r0 + tall, pl.ds(pl.multiple_of(k * WIDE, WIDE), WIDE)] = gelu_tanh(lifted).astype(BF16)
            return inner

        lax.fori_loop(0, n_up, up_step, 0)

        @pl.when(c + 2 < chunks)
        def _():
            gather.forward(c + 2)

        gather.drain(c)

        @pl.when(c >= 2)
        def _():
            second.relay(c - 2)

        def down_step(k, inner):
            weights = landed(c, k)
            at = pl.multiple_of((k - n_up) * WIDE, WIDE)
            xo_s[c, :, pl.ds(at, WIDE)] = jnp.dot(act[...], weights, preferred_element_type=F32).astype(BF16)
            return inner

        lax.fori_loop(n_up, n_tiles, down_step, 0)
        second.start(c)
        return carry

    lax.fori_loop(0, chunks, mlp_chunk, 0)

    def o_copy(c):
        return pltpu.make_async_copy(mid_s.at[c], h_out.at[pl.ds(pl.multiple_of(c * rows, rows), rows)], o_sem.at[c])

    def close(c, carry):
        @pl.when(c + 2 < chunks)
        def _():
            second.relay(c + 2)

        second.finish(c)

        def rows_at(n, inner):
            at = pl.multiple_of(n * ROW_BLOCK, ROW_BLOCK)
            mid_s[c, pl.ds(at, ROW_BLOCK), :] = (mid_s[c, pl.ds(at, ROW_BLOCK), :].astype(F32) + second.total(c, at) + bias_d).astype(BF16)
            return inner

        lax.fori_loop(0, rows // ROW_BLOCK, rows_at, 0)
        o_copy(c).start()
        return carry

    lax.fori_loop(0, chunks, close, 0)

    def settle(c, carry):
        o_copy(c).wait()
        second.drain(c)
        return carry

    lax.fori_loop(0, chunks, settle, 0)
    first.drain(chunks - 1)
    b_copy.wait_send()
    for n in range(ROLL_SLOTS):
        staged(n)


def run_block(layer, chunks, scal, q, kv_mine, kv_other, cache_mine, cache_peer, state, w_o, wo_peer, hidden, norms, b_o, b_down, b_up, up, down, up_peer, down_peer):
    model = hidden.shape[1]
    rows = hidden.shape[0] // chunks
    hd = q.shape[1]
    window = kv_mine.shape[0] // PAIR
    ffn = up_peer.shape[1]
    dims = (chunks, rows, model, hd, window, ffn)
    flops = 10 ** 11
    return pl.pallas_call(
        functools.partial(block_kernel, layer, dims),
        out_shape=(jax.ShapeDtypeStruct(hidden.shape, BF16), jax.ShapeDtypeStruct(kv_mine.shape, BF16)),
        in_specs=[SMEM] + [ANY] * 9 + [VMEM] * 4 + [ANY] * 5,
        out_specs=(ANY, ANY),
        scratch_shapes=[
            vm(PAIR * PAIR * window, WIDE),
            vm(q.shape[0] * PAIR // chunks, hd),
            vm(PAIR, PAIR * rows, KEY_TILE, dtype=F32),
            vm(rows, GROUP * hd),
            vm(GROUP * hd, model),
            vm(chunks + 1, GROUP * rows, model),
            vm(chunks, 3 * rows, model),
            vm(chunks, rows, model),
            vm(PAIR, *state.shape[1:], dtype=F32),
            vm(PAIR * ffn // WIDE, 1, WIDE, dtype=F32),
            vm(*b_up.shape),
            dma(chunks, 6),
            dma(chunks, 6),
            dma(chunks, 6),
            dma(chunks, 6),
            dma(chunks, GROUP),
            dma(chunks, GROUP),
            dma(),
            dma(),
            dma(PAIR),
            dma(),
            dma(),
            dma(PAIR),
            dma(WEIGHT_SLOTS),
            dma(),
            dma(),
            dma(chunks),
            dma(ROLL_SLOTS),
        ],
        compiler_params=pltpu.CompilerParams(vmem_limit_bytes=VMEM_LIMIT, collective_id=PAIR * layer + 1, has_side_effects=True),
        cost_estimate=pl.CostEstimate(flops=flops, bytes_accessed=90_000_000, transcendentals=0),
        name=f"block_l{layer}",
    )(scal, q, kv_mine, kv_other, cache_mine, cache_peer, state, w_o, wo_peer, hidden, norms, b_o, b_down, b_up, b_up, up, down, up_peer, down_peer)


def solution(mesh):
    row_spec = P('dp', 'tp', None)
    cache_spec = P(None, 'dp', None, 'tp', None)
    col_spec = P(None, None, 'tp')
    bias_spec = P(None, 'tp')
    in_specs = (row_spec, P('dp'), P('dp', None, None), P('dp', None, None), cache_spec, cache_spec, P('dp', None), P(), col_spec, bias_spec, col_spec, bias_spec, col_spec, bias_spec, P(None, 'tp', None), P(), col_spec, bias_spec, P(None, 'tp', None), P())
    out_specs = (row_spec, cache_spec, cache_spec, P('dp', None))

    def device_step(tokens, start_pos, cos_tab, sin_tab, key_cache, value_cache, slot_pos, norm_params, w_q, b_q, w_k, b_k, w_v, b_v, w_o, b_o, w_up, b_up, w_down, b_down):
        layers, _, window, _, hd = key_cache.shape
        cos, sin = cos_tab[0], sin_tab[0]
        kc = key_cache.reshape(layers, window, hd)
        vc = value_cache.reshape(layers, window, hd)
        hidden = tokens[0]
        fresh = []
        for layer in range(layers):
            q, kv_mine, kv_other, cache_mine, cache_peer, wo_peer, up_peer, down_peer, state = run_qkv(layer, CHUNKS, start_pos, hidden, norm_params, cos, sin, (w_q, w_k, w_v), (b_q, b_k, b_v), (kc, vc), w_o, w_up, w_down)
            hidden, kv_rolled = run_block(layer, CHUNKS, start_pos, q, kv_mine, kv_other, cache_mine, cache_peer, state, w_o, wo_peer, hidden, norm_params, b_o, b_down, b_up, w_up, w_down, up_peer, down_peer)
            fresh.append(kv_rolled)
        key_out = jnp.stack([f[:window] for f in fresh]).reshape(key_cache.shape)
        value_out = jnp.stack([f[window:] for f in fresh]).reshape(value_cache.shape)
        first_slot = start_pos[0] % window
        pos_out = (start_pos[0] + (jnp.arange(window, dtype=jnp.int32) - first_slot) % window)[None]
        return hidden[None], key_out, value_out, pos_out

    return jax.shard_map(device_step, mesh=mesh, in_specs=in_specs, out_specs=out_specs, check_vma=False)
```

time: 1040 us -> 1020 us (0.981)
  Pallas kernels: 1030 us -> 1010 us
    pallas_call x4 -> x2, Pallas kernels: 764 us -> 743 us  [run_block(): pl.pallas_call(functools.partial(block_kernel, layer, dims), out_shape=(j...]
where the time goes in v2:
time: 1020 us
  Pallas kernels  1010 us (99%)
    pallas_call x2, Pallas kernels, run_block(): pl.pallas_call(functools.partial(block_kernel, layer, dims), out_shape=(j...  743 us
    pallas_call x2, Pallas kernels, run_qkv(): pl.pallas_call(functools.partial(qkv_kernel, layer, dims), out_shape=tupl...  265 us

profile of v2, /device:TPU:0, one launch (start us, length us, event | category | flops | bytes accessed | tf_op | source)
XLA Modules:
  0.0 1021.1 jit_solution(6692706090720817873)
XLA Ops:
  1.3 133.1 %qkv_l0.1 = (bf16[8192,256]{1,0:T(8,128)(2,1)}, bf16[8192,256]{1,0:T(8,128)(2,1)}, bf16[8192,256]{1,0:T(8,128)(2,1)}, bf16[8192,256]{1,0:T(8,128)(2,1)}, bf16[81...) custom-call(s32[1]{0:T(128)} %copy.26.scal, ...), custom_call_target="tpu_custom_call" | custom-call | flops 120259084288 | bytes 20000000 | tf_op jit(solution)/shard_map/qkv_l0/pallas_call | solution.py:459
  134.3 370.5 %block_l0.1 = (bf16[512,3584]{1,0:T(8,128)(2,1)}, bf16[8192,256]{1,0:T(8,128)(2,1)}) custom-call(s32[1]{0:T(128)} %copy.26.scal, bf16[8192,256]{1,0:T(8,128)(2,1)} %get-tuple-element.26.refs_0_, bf16[8192,256]{1,0:T(8,128)(2,1)} %get-tuple-element.27.refs_1_, bf16[8192,256]{1,0:T(8,128)(2,1)} %get-tuple-element.28.refs_2_, ...), custom_call_target="tpu_custom_call" | custom-call | flops 99999997952 | bytes 90000000 | tf_op jit(solution)/shard_map/block_l0/pallas_call | solution.py:872
  504.9 131.9 %qkv_l1.1 = (bf16[8192,256]{1,0:T(8,128)(2,1)}, bf16[8192,256]{1,0:T(8,128)(2,1)}, bf16[8192,256]{1,0:T(8,128)(2,1)}, bf16[8192,256]{1,0:T(8,128)(2,1)}, bf16[81...) custom-call(s32[1]{0:T(128)} %copy.26.scal, ...), custom_call_target="tpu_custom_call" | custom-call | flops 120259084288 | bytes 20000000 | tf_op jit(solution)/shard_map/qkv_l1/pallas_call | solution.py:459
  636.7 372.2 %block_l1.1 = (bf16[512,3584]{1,0:T(8,128)(2,1)}, bf16[8192,256]{1,0:T(8,128)(2,1)}) custom-call(s32[1]{0:T(128)} %copy.26.scal, bf16[8192,256]{1,0:T(8,128)(2,1)} %get-tuple-element.36.refs_0_, bf16[8192,256]{1,0:T(8,128)(2,1)} %get-tuple-element.37.refs_1_, bf16[8192,256]{1,0:T(8,128)(2,1)} %get-tuple-element.38.refs_2_, ...), custom_call_target="tpu_custom_call" | custom-call | flops 99999997952 | bytes 90000000 | tf_op jit(solution)/shard_map/block_l1/pallas_call | solution.py:872
  1008.9 0.0 copy-start
  1008.9 2.6 slice_bitcast_fusion
  1011.5 0.8 copy-done
  1012.3 0.3 slice_bitcast_fusion.1
  1012.6 3.7 maximum_bitcast_fusion
  1016.3 0.7 fusion
  1017.0 4.1 copy.27
Async XLA Ops:
  1008.9 3.5 copy-start

commit v3 on v2

--- a/solution.py
+++ b/solution.py
@@ -296,29 +296,35 @@
             turned = jnp.concatenate([-u[:, hd // 2:], u[:, :hd // 2]], axis=1)
             return (u * t_s[c, 0, r0:r0 + n, :] + turned * t_s[c, 1, r0:r0 + n, :]).astype(BF16)
 
-        def side(g, carry):
+        def keys_values(g, carry):
+            u = jnp.dot(x_s[c, r0:r0 + n, :], w_s[PAIR * g + 1], preferred_element_type=F32) + b_s[PAIR * g + 1]
+            okv_s[pl.ds(pl.multiple_of(kv_row(c, 0, g) + r0, rows), n), :] = rope(u[:, :hd])
+            okv_s[pl.ds(pl.multiple_of(kv_row(c, 1, g) + r0, rows), n), :] = u[:, hd:].astype(BF16)
+            return carry
+
+        def for_queries(g, carry):
             u = jnp.dot(x_s[c, r0:r0 + n, :], w_s[PAIR * g], preferred_element_type=F32) + b_s[PAIR * g]
             for h in range(PAIR):
                 turned = rope(u[:, h * hd:(h + 1) * hd])
                 for i in range(count):
                     oq_s[pl.ds(pl.multiple_of(q_row(c, g, i0 + i) + h * rows, rows), rows), :] = turned[i * rows:(i + 1) * rows]
-            u = jnp.dot(x_s[c, r0:r0 + n, :], w_s[PAIR * g + 1], preferred_element_type=F32) + b_s[PAIR * g + 1]
-            okv_s[pl.ds(pl.multiple_of(kv_row(c, 0, g) + r0, rows), n), :] = rope(u[:, :hd])
-            okv_s[pl.ds(pl.multiple_of(kv_row(c, 1, g) + r0, rows), n), :] = u[:, hd:].astype(BF16)
             return carry
 
-        lax.fori_loop(0, 2, side, 0)
+        lax.fori_loop(0, PAIR, keys_values, 0)
+        for copy in kv_copies(c, range(i0, i0 + count)):
+            copy.start()
+        lax.fori_loop(0, PAIR, for_queries, 0)
 
     def q_copy(c):
         part = pl.ds(q_row(c, 0, 0), PAIR * GROUP * tall)
         return pltpu.make_async_copy(oq_s.at[part], q_out.at[part], q_sem.at[c])
 
-    def kv_copies(c):
+    def kv_copies(c, blocks):
         planes = (kv_mine, kv_other)
         made = []
         for kv in range(PAIR):
             for g in range(PAIR):
-                for i in range(GROUP):
+                for i in blocks:
                     src = okv_s.at[pl.ds(pl.multiple_of(kv_row(c, kv, g) + i * rows, rows), rows)]
                     at = pl.ds(pl.multiple_of(kv * window + chunk_pos(c, i), rows), rows)
                     made.append(pltpu.make_async_copy(src, planes[g].at[at], kv_sem.at[c]))
@@ -392,8 +398,6 @@
         gather.finish(c)
         project(c, 3, 1)
         q_copy(c).start()
-        for copy in kv_copies(c):
-            copy.start()
 
         @pl.when(c == 0)
         def _():
@@ -530,12 +534,19 @@
     load_planes(kv_mine, 3 * window, new_sem)
     load_planes(kv_other, PAIR * window, new_sem)
 
-    def pick(k):
-        return jnp.where(k == 0, 3, jnp.where(k == 3, 0, k))
+    chip = place.member(0)
+    lowest = jnp.where(chip < 2, 1, chip)
+    middle = jnp.where(jnp.logical_or(chip == 0, chip == 3), 2, 3)
+
+    def pick(c, k):
+        by_place = jnp.where(k == 0, lowest, jnp.where(k == 1, middle, 6 - lowest - middle))
+        diagonal = jnp.where(k == 0, 3, k)
+        return jnp.where(k == 3, 0, jnp.where(c == 0, by_place, diagonal))
 
     def state_copy(b):
         slot = lax.rem(b, PAIR)
-        return pltpu.make_async_copy(state.at[lax.div(b, GROUP) * GROUP + pick(lax.rem(b, GROUP))], st_s.at[slot], st_sem.at[slot])
+        c = lax.div(b, GROUP)
+        return pltpu.make_async_copy(state.at[c * GROUP + pick(c, lax.rem(b, GROUP))], st_s.at[slot], st_sem.at[slot])
 
     for b in range(PAIR):
         state_copy(jnp.int32(b)).start()
@@ -572,10 +583,10 @@
     q_copy(jnp.int32(0)).wait()
     whole(big_s.at[pl.ds(0, PAIR * window)], new_sem)
     for g in range(PAIR):
-        s_s[g] = scores(jnp.int32(0), 3, g, True, lax.div(first_row(0, 3), tile) * tile)
+        s_s[g] = scores(jnp.int32(0), lowest, g, True, lax.div(first_row(0, lowest), tile) * tile)
 
     def attend(c, k):
-        i = pick(k)
+        i = pick(c, k)
         b = c * GROUP + k
         w = lax.rem(b, PAIR)
         late = c >= EARLY
@@ -584,7 +595,7 @@
         count = jnp.where(late, tiles + 1, diag + 2)
         end = k == 3
         c_next = jnp.minimum(jnp.where(end, c + 1, c), chunks - 1)
-        i_next = pick(jnp.where(end, 0, k + 1))
+        i_next = pick(c_next, jnp.where(end, 0, k + 1))
         next_at = lax.div(first_row(c_next, i_next), tile) * tile
 
         @pl.when(late)
@@ -648,13 +659,13 @@
             cols = slice(n * WIDE, (n + 1) * WIDE)
             xo_s[c + 1, pl.ds(r0, rows), cols] = jnp.dot(mix_s[...], wo_s[:, cols], preferred_element_type=F32).astype(BF16)
 
-        @pl.when(k == 0)
+        @pl.when(i == 3)
         def _():
             first.copy(c, 0).start()
             first.copy(c, 1).start()
 
         for kind in (2, 3):
-            @pl.when(k == kind - 1)
+            @pl.when(i == kind - 1)
             def _():
                 first.copy(c, kind).start()
 
@@ -910,6 +921,45 @@
     )(scal, q, kv_mine, kv_other, cache_mine, cache_peer, state, w_o, wo_peer, hidden, norms, b_o, b_down, b_up, b_up, up, down, up_peer, down_peer)
 
 
+def copy_kernel(scal, *refs):
+    hidden, kvs = refs[0], refs[1:-8]
+    h_out, k_out, v_out, p_out, h_s, kv_s, in_sem, out_sem = refs[-8:]
+    window = k_out.shape[1]
+    cut = window // PAIR
+    part = hidden.shape[0] // PAIR
+    moves = [(hidden.at[pl.ds(n * part, part)], h_s.at[pl.ds(n * part, part)], h_out.at[pl.ds(n * part, part)]) for n in range(PAIR)]
+    for layer, kv in enumerate(kvs):
+        for k, out in enumerate((k_out, v_out)):
+            for n in range(PAIR):
+                at = pl.ds(k * window + n * cut, cut)
+                moves.append((kv.at[at], kv_s.at[layer, at], out.at[layer, pl.ds(n * cut, cut)]))
+    for n, (src, mid, _) in enumerate(moves):
+        pltpu.make_async_copy(src, mid, in_sem.at[n]).start()
+    start_pos = scal[0]
+    ahead = lax.broadcasted_iota(jnp.int32, p_out.shape, 1) + (window - lax.rem(start_pos, window))
+    p_out[...] = start_pos + jnp.where(ahead >= window, ahead - window, ahead)
+    for n, (src, mid, dst) in enumerate(moves):
+        pltpu.make_async_copy(src, mid, in_sem.at[n]).wait()
+        pltpu.make_async_copy(mid, dst, out_sem.at[n]).start()
+    for n, (_, mid, dst) in enumerate(moves):
+        pltpu.make_async_copy(mid, dst, out_sem.at[n]).wait()
+
+
+def run_copy(scal, hidden, kvs, window):
+    layers, hd = len(kvs), kvs[0].shape[1]
+    planes = jax.ShapeDtypeStruct((layers, window, hd), BF16)
+    count = PAIR + PAIR * PAIR * layers
+    return pl.pallas_call(
+        copy_kernel,
+        out_shape=(jax.ShapeDtypeStruct(hidden.shape, BF16), planes, planes, jax.ShapeDtypeStruct((1, window), jnp.int32)),
+        in_specs=[SMEM] + [ANY] * (1 + layers),
+        out_specs=(ANY, ANY, ANY, VMEM),
+        scratch_shapes=[vm(*hidden.shape), vm(layers, PAIR * window, hd), dma(count), dma(count)],
+        compiler_params=pltpu.CompilerParams(vmem_limit_bytes=VMEM_LIMIT),
+        name="copy_out",
+    )(scal, hidden, *kvs)
+
+
 def solution(mesh):
     row_spec = P('dp', 'tp', None)
     cache_spec = P(None, 'dp', None, 'tp', None)
@@ -929,10 +979,7 @@
             q, kv_mine, kv_other, cache_mine, cache_peer, wo_peer, up_peer, down_peer, state = run_qkv(layer, CHUNKS, start_pos, hidden, norm_params, cos, sin, (w_q, w_k, w_v), (b_q, b_k, b_v), (kc, vc), w_o, w_up, w_down)
             hidden, kv_rolled = run_block(layer, CHUNKS, start_pos, q, kv_mine, kv_other, cache_mine, cache_peer, state, w_o, wo_peer, hidden, norm_params, b_o, b_down, b_up, w_up, w_down, up_peer, down_peer)
             fresh.append(kv_rolled)
-        key_out = jnp.stack([f[:window] for f in fresh]).reshape(key_cache.shape)
-        value_out = jnp.stack([f[window:] for f in fresh]).reshape(value_cache.shape)
-        first_slot = start_pos[0] % window
-        pos_out = (start_pos[0] + (jnp.arange(window, dtype=jnp.int32) - first_slot) % window)[None]
-        return hidden[None], key_out, value_out, pos_out
+        hidden, key_out, value_out, pos_out = run_copy(start_pos, hidden, fresh, window)
+        return hidden[None], key_out.reshape(key_cache.shape), value_out.reshape(value_cache.shape), pos_out
 
     return jax.shard_map(device_step, mesh=mesh, in_specs=in_specs, out_specs=out_specs, check_vma=False)

time: 1020 us -> 1020 us (level)
  no operation moved by 1% of the time
where the time goes in v3:
time: 1020 us
  Pallas kernels  1020 us (100%)
    pallas_call x2, Pallas kernels, run_block(): pl.pallas_call(functools.partial(block_kernel, layer, dims), out_shape=(j...  742 us
    pallas_call x2, Pallas kernels, run_qkv(): pl.pallas_call(functools.partial(qkv_kernel, layer, dims), out_shape=tupl...  263 us

profile of v3, /device:TPU:0, one launch (start us, length us, event | category | flops | bytes accessed | tf_op | source)
XLA Modules:
  0.0 1016.6 jit_solution(12729415604199392982)
XLA Ops:
  1.3 132.2 %qkv_l0.1 = (bf16[8192,256]{1,0:T(8,128)(2,1)}, bf16[8192,256]{1,0:T(8,128)(2,1)}, bf16[8192,256]{1,0:T(8,128)(2,1)}, bf16[8192,256]{1,0:T(8,128)(2,1)}, bf16[81...) custom-call(s32[1]{0:T(128)S(6)} %copy.25.scal, ...), custom_call_target="tpu_custom_call" | custom-call | flops 120259084288 | bytes 20000000 | tf_op jit(solution)/shard_map/qkv_l0/pallas_call | solution.py:463
  133.5 371.1 %block_l0.1 = (bf16[512,3584]{1,0:T(8,128)(2,1)}, bf16[8192,256]{1,0:T(8,128)(2,1)}) custom-call(s32[1]{0:T(128)S(6)} %copy.25.scal, bf16[8192,256]{1,0:T(8,128)(2,1)} %get-tuple-element.30.refs_0_, bf16[8192,256]{1,0:T(8,128)(2,1)} %get-tuple-element.31.refs_1_, bf16[8192,256]{1,0:T(8,128)(2,1)} %get-tuple-element.32.refs_2_, ...), custom_call_target="tpu_custom_call" | custom-call | flops 99999997952 | bytes 90000000 | tf_op jit(solution)/shard_map/block_l0/pallas_call | solution.py:883
  504.5 130.9 %qkv_l1.1 = (bf16[8192,256]{1,0:T(8,128)(2,1)}, bf16[8192,256]{1,0:T(8,128)(2,1)}, bf16[8192,256]{1,0:T(8,128)(2,1)}, bf16[8192,256]{1,0:T(8,128)(2,1)}, bf16[81...) custom-call(s32[1]{0:T(128)S(6)} %copy.25.scal, ...), custom_call_target="tpu_custom_call" | custom-call | flops 120259084288 | bytes 20000000 | tf_op jit(solution)/shard_map/qkv_l1/pallas_call | solution.py:463
  635.4 371.1 %block_l1.1 = (bf16[512,3584]{1,0:T(8,128)(2,1)}, bf16[8192,256]{1,0:T(8,128)(2,1)}) custom-call(s32[1]{0:T(128)S(6)} %copy.25.scal, bf16[8192,256]{1,0:T(8,128)(2,1)} %get-tuple-element.40.refs_0_, bf16[8192,256]{1,0:T(8,128)(2,1)} %get-tuple-element.41.refs_1_, bf16[8192,256]{1,0:T(8,128)(2,1)} %get-tuple-element.42.refs_2_, ...), custom_call_target="tpu_custom_call" | custom-call | flops 99999997952 | bytes 90000000 | tf_op jit(solution)/shard_map/block_l1/pallas_call | solution.py:883
  1006.6 9.8 copy_out.1
